TPU v7x, 32 devices: a whole 2x2x4 slice. The times are simulated.
32 devices in a mesh: parts: 2 (over y), space: 4 (over z), tm: 2 (over x), spin: 2 (over core).
Axes of the slice: x: 2, y: 2, z: 4, core: 2. Of those that a mesh axis runs over, the one named last changes fastest.
Arguments:
- backward: bfloat16 [4, 2, 4, 64, 3, 4, 128], P('parts', 'tm', None, 'spin', None, 'space'), parts along dimension 0, may hold values from -6 to 6
- forward: bfloat16 [4, 2, 4, 64, 3, 4, 128], P('parts', 'tm', None, 'spin', None, 'space'), parts along dimension 0, may hold values from -6 to 6
- gauge_links: bfloat16 [4, 3, 3, 3, 2, 4, 128], P('parts', None, None, None, 'tm', 'space'), parts along dimension 0, may hold values from -2.5 to 2.5
- momenta: int32 [3, 3], replicated, may hold values from -2 to 2
- gamma_list: int32 [16], replicated, may hold values from 0 to 15
Outputs:
- insertion: float32 [4, 3, 16, 2, 64, 64], P('parts', None, None, 'tm', 'space', 'spin'), parts along dimension 0
There are 2 independent parts, one for each index of `parts`. A program takes and returns all parts, laid end to end along the dimension named above; an argument that names none is the same for every part. Nothing has to cross between parts.
All inputs are finite; a program needn't handle non-finite values.
Results may differ from a plain program's by a relative error of at most 0.0056.
Values may be sent and summed in bfloat16 or wider, within the bound.
A program may use at most 64 MiB of HBM per device.

v0:
```python
import functools
import math

import jax
import jax.numpy as jnp
import numpy as np
from jax import lax
from jax.experimental import pallas as pl
from jax.experimental.pallas import tpu as pltpu
from jax.sharding import PartitionSpec as P

LX = 32
GROUP = 16


def gamma_tables():
    zeros = np.zeros((4, 4))
    gx_imag = np.array([[0, 0, 0, 1], [0, 0, 1, 0], [0, -1, 0, 0], [-1, 0, 0, 0]]) * 1.0
    gy_real = np.array([[0, 0, 0, -1], [0, 0, 1, 0], [0, 1, 0, 0], [-1, 0, 0, 0]]) * 1.0
    gz_imag = np.array([[0, 0, 1, 0], [0, 0, 0, -1], [-1, 0, 0, 0], [0, 1, 0, 0]]) * 1.0
    gt_real = np.array([[0, 0, 1, 0], [0, 0, 0, 1], [1, 0, 0, 0], [0, 1, 0, 0]]) * 1.0
    singles = [zeros + 1j * gx_imag, gy_real + 0j, 1j * gz_imag, gt_real + 0j]
    basis = []
    for number in range(16):
        matrix = np.eye(4) + 0j
        for which in range(4):
            if number >> which & 1:
                matrix = matrix @ singles[which]
        basis.append(matrix)
    return singles, np.stack(basis)


def unit_times(unit, value):
    real, imag = value
    if unit == 1:
        return real, imag
    if unit == -1:
        return -real, -imag
    if unit == 1j:
        return -imag, real
    return imag, -real


def small_times(matrix, half):
    outs = []
    for row in range(2):
        column = int(np.flatnonzero(matrix[row])[0])
        outs.append([unit_times(complex(matrix[row, column]), value) for value in half[column]])
    return outs


def added(first, second):
    return [
        [(a[0] + b[0], a[1] + b[1]) for a, b in zip(left, right)]
        for left, right in zip(first, second)
    ]


def subtracted(first, second):
    return [
        [(a[0] - b[0], a[1] - b[1]) for a, b in zip(left, right)]
        for left, right in zip(first, second)
    ]


def kernel(
    spaces,
    width_x,
    full_z,
    scaling,
    back_hbm,
    fwd_hbm,
    link_hbm,
    momenta_ref,
    gamma_ref,
    table_ref,
    out_ref,
    chosen_ref,
    back_ref,
    fwd_ref,
    link_ref,
    other_back,
    links,
    halo_send,
    halo_recv,
    rows_scr,
    weave,
    weave_mm,
    pair,
    chunk_send,
    chunk_recv,
    load_sems,
    back_sems,
    halo_send_sems,
    halo_recv_sems,
    chunk_send_sems,
    chunk_recv_sems,
):
    loads = [
        pltpu.make_async_copy(source, target, load_sems.at[number])
        for number, (source, target) in enumerate(
            ((fwd_hbm, fwd_ref), (link_hbm, link_ref), (back_hbm, back_ref))
        )
    ]
    for load in loads:
        load.start()
    columns = fwd_ref.shape[3]
    plane = fwd_ref.shape[4]
    moments = momenta_ref.shape[0]
    here = lax.axis_index("space")
    core = lax.axis_index("spin")
    after = lax.rem(here + 1, spaces)
    before = lax.rem(here + spaces - 1, spaces)
    singles, _ = gamma_tables()

    barrier = pltpu.get_barrier_semaphore()
    pl.semaphore_signal(barrier, inc=1, device_id={"spin": 1 - core})
    for step in range(1, spaces):
        pl.semaphore_signal(
            barrier, inc=1, device_id={"space": lax.rem(here + step, spaces)}
        )

    for load in loads[:2]:
        load.wait()
    for mu in range(3):
        for c in range(3):
            for d in range(3):
                row = ((mu * 3 + c) * 3 + d) * 2
                links[row : row + 2, :] = link_ref[mu, c, d].astype(jnp.float32)

    def link(mu, c, d):
        row = ((mu * 3 + c) * 3 + d) * 2
        return [
            jnp.broadcast_to(links[row + part : row + part + 1, :], (GROUP, plane))
            for part in range(2)
        ]

    def colour(mu, half, dagger):
        outs = [[None] * 3 for _ in range(2)]
        for c in range(3):
            for d in range(3):
                u_real, u_imag = link(mu, d, c) if dagger else link(mu, c, d)
                for spin in range(2):
                    v_real, v_imag = half[spin][d]
                    if dagger:
                        real = u_real * v_real + u_imag * v_imag
                        imag = u_real * v_imag - u_imag * v_real
                    else:
                        real = u_real * v_real - u_imag * v_imag
                        imag = u_real * v_imag + u_imag * v_real
                    held = outs[spin][c]
                    outs[spin][c] = (
                        (real, imag) if held is None else (held[0] + real, held[1] + imag)
                    )
        return outs

    lanes = lax.broadcasted_iota(jnp.int32, (GROUP, plane), 1)
    column_x = lax.rem(lanes, width_x)

    def rolled(value, steps, along_y):
        if along_y:
            return pltpu.roll(value, (steps * width_x) % plane, 1)
        plain = pltpu.roll(value, steps % plane, 1)
        wrapped = pltpu.roll(value, (steps - steps * width_x) % plane, 1)
        edge = 0 if steps == 1 else width_x - 1
        return jnp.where(column_x == edge, wrapped, plain)

    def rolled_half(half, steps, along_y):
        return [
            [tuple(rolled(part, steps, along_y) for part in value) for value in spin]
            for spin in half
        ]

    def spinor(cols):
        return [
            [
                tuple(fwd_ref[part, s, c, cols, :].astype(jnp.float32) for part in range(2))
                for c in range(3)
            ]
            for s in range(4)
        ]

    def group(index):
        return pl.ds(pl.multiple_of(index * GROUP, GROUP), GROUP)

    def halo_group(index, carry):
        cols = group(index)
        psi = spinor(cols)
        turned = small_times(singles[2][:2, 2:], psi[2:])
        minus = subtracted(psi[:2], turned)
        plus = colour(2, added(psi[:2], turned), True)
        for side, half in enumerate((minus, plus)):
            for spin in range(2):
                for c in range(3):
                    for part in range(2):
                        halo_send[side, part, spin, c, cols, :] = half[spin][c][part].astype(
                            jnp.bfloat16
                        )
        return carry

    lax.fori_loop(0, columns // GROUP, halo_group, 0)

    pl.semaphore_wait(barrier, spaces)

    halo_copies = []
    for side, target in ((0, before), (1, after)):
        copy = pltpu.make_async_remote_copy(
            src_ref=halo_send.at[side],
            dst_ref=halo_recv.at[side],
            send_sem=halo_send_sems.at[side],
            recv_sem=halo_recv_sems.at[side],
            device_id={"space": target},
        )
        copy.start()
        halo_copies.append(copy)
    loads[2].wait()
    back_copy = pltpu.make_async_remote_copy(
        src_ref=back_ref,
        dst_ref=other_back,
        send_sem=back_sems.at[0],
        recv_sem=back_sems.at[1],
        device_id={"spin": 1 - core},
    )
    back_copy.start()

    def store_weave(cols, full, first):
        for s in range(4):
            for c in range(3):
                for part in range(2):
                    value = full[s][c][part]
                    if not first:
                        value = value + weave[part, s, c, cols, :]
                    weave[part, s, c, cols, :] = value

    def plane_group(index, carry):
        cols = group(index)
        psi = spinor(cols)
        upper = lower = None
        for mu in range(2):
            turned = small_times(singles[mu][:2, 2:], psi[2:])
            ahead = colour(mu, rolled_half(subtracted(psi[:2], turned), -1, mu == 1), False)
            behind = rolled_half(colour(mu, added(psi[:2], turned), True), 1, mu == 1)
            up = subtracted(ahead, behind)
            low = small_times(-singles[mu][2:, :2], added(ahead, behind))
            upper = up if upper is None else added(upper, up)
            lower = low if lower is None else added(lower, low)
        store_weave(cols, upper + lower, True)
        return carry

    lax.fori_loop(0, columns // GROUP, plane_group, 0)

    sites = lax.broadcasted_iota(jnp.int32, (8, plane), 1)
    coord_x = lax.rem(sites, width_x).astype(jnp.float32)
    coord_y = lax.div(sites, width_x).astype(jnp.float32)
    coord_z = here.astype(jnp.float32)
    phases = []
    for number in range(moments):
        momentum = [momenta_ref[number, axis].astype(jnp.float32) for axis in range(3)]
        turns = coord_x * (momentum[0] * (1.0 / width_x))
        turns = turns + coord_y * (momentum[1] * (width_x / plane))
        turns = turns + coord_z * (momentum[2] * (1.0 / full_z))
        theta = (2.0 * math.pi) * (turns - jnp.floor(turns))
        phases.append((jnp.cos(theta)[:1, :], jnp.sin(theta)[:1, :]))

    def arrange(half, source):
        rows = columns * 2 // spaces
        local = columns // rows
        for part in range(2):
            for c in range(3):
                lane = (part * 3 + c) * plane
                for s in range(4):
                    for j in range(local):
                        row = half * 4 * columns + (j * 4 + s) * rows
                        rows_scr[row : row + rows, lane : lane + plane] = source[
                            part, s, c, j * rows : (j + 1) * rows, :
                        ]

    arrange(0, back_ref)

    back_copy.wait_recv()
    arrange(1, other_back)

    for copy in halo_copies:
        copy.wait_recv()

    def depth_group(index, carry):
        cols = group(index)
        received = [
            [
                [
                    tuple(
                        halo_recv[side, part, spin, c, cols, :].astype(jnp.float32)
                        for part in range(2)
                    )
                    for c in range(3)
                ]
                for spin in range(2)
            ]
            for side in range(2)
        ]
        ahead = colour(2, received[0], False)
        behind = received[1]
        upper = subtracted(ahead, behind)
        lower = small_times(-singles[2][2:, :2], added(ahead, behind))
        store_weave(cols, upper + lower, False)
        return carry

    lax.fori_loop(0, columns // GROUP, depth_group, 0)

    local_chunks = spaces // 2
    chunk_rows = 4 * columns // local_chunks
    copies = {}
    for number in range(moments):
        cosine, sine = phases[number]
        for s in range(4):
            for c in range(3):
                real = weave[0, s, c]
                imag = weave[1, s, c]
                turned_real = (cosine * real + sine * imag).astype(jnp.bfloat16)
                turned_imag = (cosine * imag - sine * real).astype(jnp.bfloat16)
                rows_at = slice(s * columns, (s + 1) * columns)
                rows_next = slice((4 + s) * columns, (5 + s) * columns)
                lanes_at = slice(c * plane, (c + 1) * plane)
                lanes_next = slice((3 + c) * plane, (4 + c) * plane)
                weave_mm[number, rows_at, lanes_at] = turned_real
                weave_mm[number, rows_at, lanes_next] = turned_imag
                weave_mm[number, rows_next, lanes_at] = turned_imag
                weave_mm[number, rows_next, lanes_next] = -turned_real
        product = lax.dot_general(
            rows_scr[...],
            weave_mm[number],
            (((1,), (1,)), ((), ())),
            preferred_element_type=jnp.float32,
        )
        for half in range(2):
            owner = core if half == 0 else 1 - core
            for j in range(local_chunks):
                target = owner * local_chunks + j
                top = (half * local_chunks + j) * chunk_rows
                for part in range(2):
                    piece = product[
                        top : top + chunk_rows, part * 4 * columns : (part + 1) * 4 * columns
                    ]
                    pair[number, target, part] = piece
                    chunk_send[number, target, part] = piece.astype(jnp.bfloat16)

        if number > 0:
            send_chunks(number - 1, spaces, here, chunk_send, chunk_recv, chunk_send_sems,
                        chunk_recv_sems, copies)
    for k in range(gamma_ref.shape[0]):
        chosen_ref[k] = table_ref[gamma_ref[k]]
    send_chunks(moments - 1, spaces, here, chunk_send, chunk_recv, chunk_send_sems,
                chunk_recv_sems, copies)

    for number in range(moments):
        total = [pair[number, here, part] for part in range(2)]
        for step in range(1, spaces):
            copies[number, step].wait_recv()
            for part in range(2):
                total[part] = total[part] + chunk_recv[number, step - 1, part].astype(
                    jnp.float32
                )
        for part in range(2):
            out_ref[number, part] = total[part] * scaling

    back_copy.wait_send()
    for copy in halo_copies:
        copy.wait_send()
    for copy in copies.values():
        copy.wait_send()


def insert_kernel(chosen_ref, pair_ref, out_hbm, out_ref, sems):
    moments, gammas, rows, columns = out_ref.shape[1:]
    stores = []
    for number in range(moments):
        spins = [
            [pair_ref[number, part, s * rows : (s + 1) * rows, :] for s in range(4)]
            for part in range(2)
        ]
        for k in range(gammas):
            real = imag = None
            for s in range(4):
                g_real = chosen_ref[k, s : s + 1, :]
                g_imag = chosen_ref[k, 4 + s : 5 + s, :]
                one = g_real * spins[0][s] - g_imag * spins[1][s]
                two = g_real * spins[1][s] + g_imag * spins[0][s]
                real = one if real is None else real + one
                imag = two if imag is None else imag + two
            for part, value in enumerate((real, imag)):
                summed = value[:, :columns]
                for other in range(1, 4):
                    summed = summed + value[:, other * columns : (other + 1) * columns]
                out_ref[part, number, k] = summed
        stores.append(
            pltpu.make_async_copy(out_ref.at[:, number], out_hbm.at[:, number], sems.at[number])
        )
        if number > 0:
            stores[number - 1].start()
    stores[-1].start()
    for store in stores:
        store.wait()


def send_chunks(
    number, spaces, here, chunk_send, chunk_recv, chunk_send_sems, chunk_recv_sems, copies
):
    for step in sorted(range(1, spaces), key=lambda step: -min(step, spaces - step)):
        target = lax.rem(here + step, spaces)
        copy = pltpu.make_async_remote_copy(
            src_ref=chunk_send.at[number, target],
            dst_ref=chunk_recv.at[number, step - 1],
            send_sem=chunk_send_sems.at[number, step - 1],
            recv_sem=chunk_recv_sems.at[number, step - 1],
            device_id={"space": target},
        )
        copy.start()
        copies[number, step] = copy


def body(mesh, backward, forward, gauge_links, momenta, gamma_list):
    spaces = mesh.shape["space"]
    _, times, _, columns, _, layers, plane = forward.shape
    moments = momenta.shape[0]
    gammas = gamma_list.shape[0]
    rows = columns * mesh.shape["spin"] // spaces
    back = jnp.transpose(backward, (0, 1, 2, 4, 5, 3, 6)).reshape(2, 4, 3, columns, plane)
    fwd = jnp.transpose(forward, (0, 1, 2, 4, 5, 3, 6)).reshape(2, 4, 3, columns, plane)
    link = jnp.transpose(gauge_links, (1, 2, 3, 4, 5, 0, 6)).reshape(3, 3, 3, 2, plane)
    full_z = layers * spaces
    scaling = 0.5 / math.sqrt(3.0 * plane * full_z)
    _, basis = gamma_tables()
    table = np.concatenate([basis.real, basis.imag], axis=1)
    table = np.repeat(table, columns, axis=2).astype(np.float32)
    vmem = pl.BlockSpec(memory_space=pltpu.VMEM)
    anywhere = pl.BlockSpec(memory_space=pl.ANY)
    smem = pl.BlockSpec(memory_space=pltpu.SMEM)
    pairs, chosen = pl.pallas_call(
        functools.partial(kernel, spaces, LX, full_z, scaling),
        out_shape=[
            pltpu.VMEM((moments, 2, 4 * rows, 4 * columns), jnp.float32),
            pltpu.VMEM((gammas,) + table.shape[1:], jnp.float32),
        ],
        in_specs=[anywhere, anywhere, anywhere, smem, smem, vmem],
        out_specs=[vmem, vmem],
        scratch_shapes=[
            pltpu.VMEM(back.shape, back.dtype),
            pltpu.VMEM(fwd.shape, fwd.dtype),
            pltpu.VMEM(link.shape, link.dtype),
            pltpu.VMEM((2, 4, 3, columns, plane), jnp.bfloat16),
            pltpu.VMEM((56, plane), jnp.float32),
            pltpu.VMEM((2, 2, 2, 3, columns, plane), jnp.bfloat16),
            pltpu.VMEM((2, 2, 2, 3, columns, plane), jnp.bfloat16),
            pltpu.VMEM((8 * columns, 6 * plane), jnp.bfloat16),
            pltpu.VMEM((2, 4, 3, columns, plane), jnp.float32),
            pltpu.VMEM((moments, 8 * columns, 6 * plane), jnp.bfloat16),
            pltpu.VMEM((moments, spaces, 2, 4 * rows, 4 * columns), jnp.float32),
            pltpu.VMEM((moments, spaces, 2, 4 * rows, 4 * columns), jnp.bfloat16),
            pltpu.VMEM((moments, spaces - 1, 2, 4 * rows, 4 * columns), jnp.bfloat16),
            pltpu.SemaphoreType.DMA((3,)),
            pltpu.SemaphoreType.DMA((2,)),
            pltpu.SemaphoreType.DMA((2,)),
            pltpu.SemaphoreType.DMA((2,)),
            pltpu.SemaphoreType.DMA((moments, spaces - 1)),
            pltpu.SemaphoreType.DMA((moments, spaces - 1)),
        ],
        compiler_params=pltpu.CompilerParams(collective_id=0, has_side_effects=True),
    )(back, fwd, link, momenta, gamma_list, table)
    out_shape = (2, moments, gammas, rows, columns)
    out = pl.pallas_call(
        insert_kernel,
        out_shape=jax.ShapeDtypeStruct(out_shape, jnp.float32),
        in_specs=[vmem, vmem],
        out_specs=anywhere,
        scratch_shapes=[
            pltpu.VMEM(out_shape, jnp.float32),
            pltpu.SemaphoreType.DMA((moments,)),
        ],
    )(
        pltpu.with_memory_space_constraint(chosen, pltpu.VMEM),
        pltpu.with_memory_space_constraint(pairs, pltpu.VMEM),
    )
    return out.reshape(2, moments, gammas, times, rows, columns)


def solution(mesh):
    in_specs = (
        P("parts", "tm", None, "spin", None, "space", None),
        P("parts", "tm", None, "spin", None, "space", None),
        P("parts", None, None, None, "tm", "space", None),
        P(),
        P(),
    )
    out_specs = P("parts", None, None, "tm", "space", "spin")
    return jax.shard_map(
        functools.partial(body, mesh),
        mesh=mesh,
        in_specs=in_specs,
        out_specs=out_specs,
        check_vma=False,
    )
```

profile of v0, /device:TPU:0, one launch (start us, length us, event | category | flops | bytes accessed | tf_op | source)
XLA Modules:
  0.0 22.2 jit_solution(1695677846175700564)
XLA Ops:
  0.0 20.7 %shard_map.64 = (f32[3,2,64,128]{3,2,1,0:T(8,128)S(1)}, f32[16,8,128]{2,1,0:T(8,128)S(1)}) custom-call(bf16[2,4,3,32,128]{4,3,2,1,0:T(8,128)(2,1)} %bitcast.18, bf16[2,4,3,32,128]{4,3,2,1,0:T(8,128)(2,1)} %bitcast.19, bf16[3,3,3,2,128]{4,3,2,1,0:T(2,128)(2,1)} %bitcast.20, s32[3,3]{1,0:T(4,128)} %momenta_ref.1, s32[16]{0:T(128)} %gamma_ref.1, ...), custom_call_target="tpu_custom_call" | custom-call | tf_op jit(solution)/shard_map/pallas_call | solution.py:438
  20.7 1.5 %shard_map.65 = f32[2,3,16,16,32]{4,3,2,1,0:T(8,128)} custom-call(f32[16,8,128]{2,1,0:T(8,128)S(1)} %get-tuple-element.7.chosen_ref, f32[3,2,64,128]{3,2,1,0:T(8,128)S(1)} %get-tuple-element.8.pair_ref), custom_call_target="tpu_custom_call" | custom-call | tf_op jit(solution)/shard_map/pallas_call | solution.py:470
where the time goes:
time: 22.4 us; the launch traced here: 22.2 us
  Pallas kernels  22.2 us (99%)
    pallas_call x1, Pallas kernels, body(): pl.pallas_call(functools.partial(kernel, spaces, LX, full_z, scaling), ou...  20.7 us
    pallas_call x1, Pallas kernels, body(): pl.pallas_call(insert_kernel, out_shape=jax.ShapeDtypeStruct(out_shape, j...  1.5 us

commit v1 on v0

v1 whole, which is shorter than its diff:
```python
import functools
import math

import jax
import jax.numpy as jnp
import numpy as np
from jax import lax
from jax.experimental import pallas as pl
from jax.experimental.pallas import tpu as pltpu
from jax.sharding import PartitionSpec as P

LX = 32
GROUP = 16
LINE = 4


def gamma_tables():
    zeros = np.zeros((4, 4))
    gx_imag = np.array([[0, 0, 0, 1], [0, 0, 1, 0], [0, -1, 0, 0], [-1, 0, 0, 0]]) * 1.0
    gy_real = np.array([[0, 0, 0, -1], [0, 0, 1, 0], [0, 1, 0, 0], [-1, 0, 0, 0]]) * 1.0
    gz_imag = np.array([[0, 0, 1, 0], [0, 0, 0, -1], [-1, 0, 0, 0], [0, 1, 0, 0]]) * 1.0
    gt_real = np.array([[0, 0, 1, 0], [0, 0, 0, 1], [1, 0, 0, 0], [0, 1, 0, 0]]) * 1.0
    singles = [zeros + 1j * gx_imag, gy_real + 0j, 1j * gz_imag, gt_real + 0j]
    basis = []
    for number in range(16):
        matrix = np.eye(4) + 0j
        for which in range(4):
            if number >> which & 1:
                matrix = matrix @ singles[which]
        basis.append(matrix)
    return singles, np.stack(basis)


def unit_times(unit, value):
    real, imag = value
    if unit == 1:
        return real, imag
    if unit == -1:
        return -real, -imag
    if unit == 1j:
        return -imag, real
    return imag, -real


def small_times(matrix, half):
    outs = []
    for row in range(2):
        column = int(np.flatnonzero(matrix[row])[0])
        outs.append([unit_times(complex(matrix[row, column]), value) for value in half[column]])
    return outs


def added(first, second):
    return [
        [(a[0] + b[0], a[1] + b[1]) for a, b in zip(left, right)]
        for left, right in zip(first, second)
    ]


def subtracted(first, second):
    return [
        [(a[0] - b[0], a[1] - b[1]) for a, b in zip(left, right)]
        for left, right in zip(first, second)
    ]


def kernel(
    spaces,
    width_x,
    full_z,
    back_hbm,
    fwd_hbm,
    link_hbm,
    momenta_ref,
    gamma_ref,
    table_hbm,
    out_ref,
    back_ref,
    fwd_ref,
    link_ref,
    table_ref,
    other_back,
    chosen_ref,
    links,
    halo_send,
    halo_recv,
    rows_scr,
    weave,
    weave_mm,
    pair,
    chunk_send,
    chunk_recv,
    load_sems,
    back_sems,
    halo_send_sems,
    halo_recv_sems,
    chunk_send_sems,
    chunk_recv_sems,
    ready_sem,
):
    loads = [
        pltpu.make_async_copy(source, target, load_sems.at[number])
        for number, (source, target) in enumerate(
            (
                (fwd_hbm, fwd_ref),
                (link_hbm, link_ref),
                (back_hbm, back_ref),
                (table_hbm, table_ref),
            )
        )
    ]
    for load in loads:
        load.start()
    columns = fwd_ref.shape[3]
    plane = fwd_ref.shape[4]
    moments = momenta_ref.shape[0]
    gammas = gamma_ref.shape[0]
    groups = columns // GROUP
    rows = columns * 2 // spaces
    last = spaces - 1
    relayed = 4 <= spaces <= LINE
    here = lax.axis_index("space")
    core = lax.axis_index("spin")
    after = lax.rem(here + 1, spaces)
    before = lax.rem(here + last, spaces)
    singles, _ = gamma_tables()

    barrier = pltpu.get_barrier_semaphore()
    for step in range(1, spaces):
        pl.semaphore_signal(
            barrier, inc=1, device_id={"space": lax.rem(here + step, spaces)}
        )

    @pl.when(core == 0)
    def _():
        pl.semaphore_signal(barrier, inc=1, device_id={"spin": 1 - core})

    if relayed:
        for g in range(groups):
            for number in range(moments):

                @pl.when(here == 0)
                def _(g=g, number=number):
                    chunk_recv[g, number, 0] = jnp.zeros_like(chunk_recv[g, number, 0])

                @pl.when(here == last)
                def _(g=g, number=number):
                    chunk_recv[g, number, last - 1] = jnp.zeros_like(chunk_recv[g, number, 0])

    for load in loads[:2]:
        load.wait()
    for mu in range(3):
        for c in range(3):
            for d in range(3):
                row = ((mu * 3 + c) * 3 + d) * 2
                links[row : row + 2, :] = link_ref[mu, c, d].astype(jnp.float32)

    def link(mu, c, d):
        row = ((mu * 3 + c) * 3 + d) * 2
        return [
            jnp.broadcast_to(links[row + part : row + part + 1, :], (GROUP, plane))
            for part in range(2)
        ]

    def colour(mu, half, dagger):
        outs = [[None] * 3 for _ in range(2)]
        for c in range(3):
            for d in range(3):
                u_real, u_imag = link(mu, d, c) if dagger else link(mu, c, d)
                for spin in range(2):
                    v_real, v_imag = half[spin][d]
                    if dagger:
                        real = u_real * v_real + u_imag * v_imag
                        imag = u_real * v_imag - u_imag * v_real
                    else:
                        real = u_real * v_real - u_imag * v_imag
                        imag = u_real * v_imag + u_imag * v_real
                    held = outs[spin][c]
                    outs[spin][c] = (
                        (real, imag) if held is None else (held[0] + real, held[1] + imag)
                    )
        return outs

    lanes = lax.broadcasted_iota(jnp.int32, (GROUP, plane), 1)
    column_x = lax.rem(lanes, width_x)

    def rolled(value, steps, along_y):
        if along_y:
            return pltpu.roll(value, (steps * width_x) % plane, 1)
        plain = pltpu.roll(value, steps % plane, 1)
        wrapped = pltpu.roll(value, (steps - steps * width_x) % plane, 1)
        edge = 0 if steps == 1 else width_x - 1
        return jnp.where(column_x == edge, wrapped, plain)

    def rolled_half(half, steps, along_y):
        return [
            [tuple(rolled(part, steps, along_y) for part in value) for value in spin]
            for spin in half
        ]

    def spinor(cols):
        return [
            [
                tuple(fwd_ref[part, s, c, cols, :].astype(jnp.float32) for part in range(2))
                for c in range(3)
            ]
            for s in range(4)
        ]

    def group(index):
        if isinstance(index, int):
            return slice(index * GROUP, (index + 1) * GROUP)
        return pl.ds(pl.multiple_of(index * GROUP, GROUP), GROUP)

    def halo_copy(g, side):
        return pltpu.make_async_remote_copy(
            src_ref=halo_send.at[g, side],
            dst_ref=halo_recv.at[g, side],
            send_sem=halo_send_sems.at[g, side],
            recv_sem=halo_recv_sems.at[g, side],
            device_id={"space": before if side == 0 else after},
        )

    for g in range(groups):
        psi = spinor(group(g))
        turned = small_times(singles[2][:2, 2:], psi[2:])
        minus = subtracted(psi[:2], turned)
        plus = colour(2, added(psi[:2], turned), True)
        for side, half in enumerate((minus, plus)):
            for spin in range(2):
                for c in range(3):
                    for part in range(2):
                        halo_send[g, side, part, spin, c] = half[spin][c][part].astype(
                            jnp.bfloat16
                        )
        if g == 0:
            pl.semaphore_wait(barrier, last + core)

        @pl.when(here == last)
        def _(g=g):
            halo_copy(g, 1).start()
            halo_copy(g, 0).start()

        @pl.when(here != last)
        def _(g=g):
            halo_copy(g, 0).start()
            halo_copy(g, 1).start()

    loads[2].wait()
    back_copy = pltpu.make_async_remote_copy(
        src_ref=back_ref,
        dst_ref=other_back,
        send_sem=back_sems.at[0],
        recv_sem=back_sems.at[1],
        device_id={"spin": 1 - core},
    )

    @pl.when(core == 1)
    def _():
        pl.semaphore_signal(ready_sem, inc=1, device_id={"spin": 1 - core})
        back_copy.start()

    def store_weave(cols, full, first):
        for s in range(4):
            for c in range(3):
                for part in range(2):
                    value = full[s][c][part]
                    if not first:
                        value = value + weave[part, s, c, cols, :]
                    weave[part, s, c, cols, :] = value

    def plane_group(index, carry):
        cols = group(index)
        psi = spinor(cols)
        upper = lower = None
        for mu in range(2):
            turned = small_times(singles[mu][:2, 2:], psi[2:])
            ahead = colour(mu, rolled_half(subtracted(psi[:2], turned), -1, mu == 1), False)
            behind = rolled_half(colour(mu, added(psi[:2], turned), True), 1, mu == 1)
            up = subtracted(ahead, behind)
            low = small_times(-singles[mu][2:, :2], added(ahead, behind))
            upper = up if upper is None else added(upper, up)
            lower = low if lower is None else added(lower, low)
        store_weave(cols, upper + lower, True)
        return carry

    lax.fori_loop(0, groups, plane_group, 0)

    sites = lax.broadcasted_iota(jnp.int32, (8, plane), 1)
    coord_x = lax.rem(sites, width_x).astype(jnp.float32)
    coord_y = lax.div(sites, width_x).astype(jnp.float32)
    coord_z = here.astype(jnp.float32)
    phases = []
    for number in range(moments):
        momentum = [momenta_ref[number, axis].astype(jnp.float32) for axis in range(3)]
        turns = coord_x * (momentum[0] * (1.0 / width_x))
        turns = turns + coord_y * (momentum[1] * (width_x / plane))
        turns = turns + coord_z * (momentum[2] * (1.0 / full_z))
        theta = (2.0 * math.pi) * (turns - jnp.floor(turns))
        phases.append((jnp.cos(theta)[:1, :], jnp.sin(theta)[:1, :]))

    loads[3].wait()
    for k in range(gammas):
        chosen_ref[k] = table_ref[gamma_ref[k]]

    def arrange(owner, source):
        for part in range(2):
            for c in range(3):
                lane = (part * 3 + c) * plane
                for s in range(4):
                    for j in range(columns // rows):
                        row = (j * 4 + s) * rows
                        rows_scr[owner, row : row + rows, lane : lane + plane] = source[
                            part, s, c, j * rows : (j + 1) * rows, :
                        ]

    arrange(core, back_ref)

    @pl.when(core == 0)
    def _():
        pl.semaphore_wait(ready_sem, 1)
        back_copy.start()

    back_copy.wait_recv()
    arrange(1 - core, other_back)

    def is_long(step):
        if not relayed or step not in (1, last):
            return None
        return here == (last if step == 1 else 0)

    inner = (here != 0) & (here != last)
    far = jnp.where(here == 1, last, 0)

    def chunk_copy(g, number, step):
        target = source = lax.rem(here + step, spaces)
        slot = step - 1
        long = is_long(step)
        if long is not None:
            target = jnp.where(long, last - 1 if step == 1 else 1, target)
            slot = jnp.where(long, last, slot)
        return pltpu.make_async_remote_copy(
            src_ref=chunk_send.at[g, number, source],
            dst_ref=chunk_recv.at[g, number, slot],
            send_sem=chunk_send_sems.at[g, number, step - 1],
            recv_sem=chunk_recv_sems.at[g, number, slot],
            device_id={"space": target},
        )

    def wait_chunk(g, number, slot):
        pltpu.make_async_remote_copy(
            src_ref=chunk_send.at[g, number, 0],
            dst_ref=chunk_recv.at[g, number, slot],
            send_sem=chunk_send_sems.at[g, number, 0],
            recv_sem=chunk_recv_sems.at[g, number, slot],
            device_id={"space": after},
        ).wait_recv()

    chunk_rows = 4 * rows
    order = sorted(range(1, spaces), key=lambda step: -min(step, spaces - step))
    if relayed:
        order = [last, 1] + [step for step in order if step not in (1, last)]
    for g in range(groups):
        for side in range(2):
            halo_copy(g, side).wait_recv()
        received = [
            [
                [
                    tuple(
                        halo_recv[g, side, part, spin, c].astype(jnp.float32)
                        for part in range(2)
                    )
                    for c in range(3)
                ]
                for spin in range(2)
            ]
            for side in range(2)
        ]
        ahead = colour(2, received[0], False)
        behind = received[1]
        upper = subtracted(ahead, behind)
        lower = small_times(-singles[2][2:, :2], added(ahead, behind))
        cols = group(g)
        store_weave(cols, upper + lower, False)
        for number in range(moments):
            cosine, sine = phases[number]
            for s in range(4):
                for c in range(3):
                    real = weave[0, s, c, cols, :]
                    imag = weave[1, s, c, cols, :]
                    turned_real = (cosine * real + sine * imag).astype(jnp.bfloat16)
                    turned_imag = (cosine * imag - sine * real).astype(jnp.bfloat16)
                    rows_at = slice(s * GROUP, (s + 1) * GROUP)
                    rows_next = slice((4 + s) * GROUP, (5 + s) * GROUP)
                    lanes_at = slice(c * plane, (c + 1) * plane)
                    lanes_next = slice((3 + c) * plane, (4 + c) * plane)
                    weave_mm[g, number, rows_at, lanes_at] = turned_real
                    weave_mm[g, number, rows_at, lanes_next] = turned_imag
                    weave_mm[g, number, rows_next, lanes_at] = turned_imag
                    weave_mm[g, number, rows_next, lanes_next] = -turned_real
            product = lax.dot_general(
                rows_scr[...].reshape(8 * columns, 6 * plane),
                weave_mm[g, number],
                (((1,), (1,)), ((), ())),
                preferred_element_type=jnp.float32,
            )
            for target in range(spaces):
                piece = product[target * chunk_rows : (target + 1) * chunk_rows]
                pair[g, number, target] = piece
                chunk_send[g, number, target] = piece.astype(jnp.bfloat16)
            for step in order:
                copy = chunk_copy(g, number, step)
                if relayed and 1 < step < last:
                    delayed = inner & (lax.rem(here + step, spaces) == far)
                    pl.when(jnp.logical_not(delayed))(copy.start)
                else:
                    copy.start()

    if relayed:
        for g in range(groups):
            for number in range(moments):
                for step in range(2, last):

                    @pl.when(((here == 1) & (step == last - 1)) | ((here == last - 1) & (step == 2)))
                    def _(g=g, number=number, step=step):
                        wait_chunk(g, number, last)
                        target = lax.rem(here + step, spaces)
                        summed = pair[g, number, target] + chunk_recv[g, number, last].astype(
                            jnp.float32
                        )
                        chunk_send[g, number, target] = summed.astype(jnp.bfloat16)
                        chunk_copy(g, number, step).start()

    width = pair.shape[-1]
    half = width // 2
    for g in range(groups):
        for number in range(moments):
            total = pair[g, number, here]
            for step in range(1, spaces):
                if relayed and step in (1, last):
                    end = 0 if step == 1 else last
                    pl.when(here != end)(
                        functools.partial(wait_chunk, g, number, step - 1)
                    )
                else:
                    wait_chunk(g, number, step - 1)
                total = total + chunk_recv[g, number, step - 1].astype(jnp.float32)
            values = [total[s * rows : (s + 1) * rows] for s in range(4)]
            turned = [pltpu.roll(value, half, 1) for value in values]
            for k in range(gammas):
                summed = None
                for s in range(4):
                    term = chosen_ref[k, s : s + 1, :] * values[s]
                    term = term + chosen_ref[k, 4 + s : 5 + s, :] * turned[s]
                    summed = term if summed is None else summed + term
                summed = summed + pltpu.roll(summed, width - GROUP, 1)
                summed = summed + pltpu.roll(summed, width - 2 * GROUP, 1)
                for part in range(2):
                    out_ref[part, number, k, :, g * GROUP : (g + 1) * GROUP] = summed[
                        :, part * half : part * half + GROUP
                    ]

    back_copy.wait_send()
    for g in range(groups):
        for side in range(2):
            halo_copy(g, side).wait_send()
        for number in range(moments):
            for step in range(1, spaces):
                chunk_copy(g, number, step).wait_send()


def store_kernel(value_ref, out_hbm, sems):
    moments = value_ref.shape[1]
    stores = [
        pltpu.make_async_copy(
            value_ref.at[:, number], out_hbm.at[:, number], sems.at[number]
        )
        for number in range(moments)
    ]
    for store in stores:
        store.start()
    for store in stores:
        store.wait()


def body(mesh, backward, forward, gauge_links, momenta, gamma_list):
    spaces = mesh.shape["space"]
    _, times, _, columns, _, layers, plane = forward.shape
    moments = momenta.shape[0]
    gammas = gamma_list.shape[0]
    rows = columns * mesh.shape["spin"] // spaces
    groups = columns // GROUP
    back = jnp.transpose(backward, (0, 1, 2, 4, 5, 3, 6)).reshape(2, 4, 3, columns, plane)
    fwd = jnp.transpose(forward, (0, 1, 2, 4, 5, 3, 6)).reshape(2, 4, 3, columns, plane)
    link = jnp.transpose(gauge_links, (1, 2, 3, 4, 5, 0, 6)).reshape(3, 3, 3, 2, plane)
    full_z = layers * spaces
    scaling = 0.5 / math.sqrt(3.0 * plane * full_z)
    _, basis = gamma_tables()
    plain = np.concatenate([basis.real, basis.real], axis=2)
    crossed = np.concatenate([-basis.imag, basis.imag], axis=2)
    table = np.concatenate([plain, crossed], axis=1)
    table = (np.repeat(table, GROUP, axis=2) * scaling).astype(np.float32)
    width = table.shape[2]
    slots = spaces if 4 <= spaces <= LINE else spaces - 1
    vmem = pl.BlockSpec(memory_space=pltpu.VMEM)
    anywhere = pl.BlockSpec(memory_space=pl.ANY)
    smem = pl.BlockSpec(memory_space=pltpu.SMEM)
    out_shape = (2, moments, gammas, rows, columns)
    values = pl.pallas_call(
        functools.partial(kernel, spaces, LX, full_z),
        out_shape=pltpu.VMEM(out_shape, jnp.float32),
        in_specs=[anywhere, anywhere, anywhere, smem, smem, anywhere],
        out_specs=vmem,
        scratch_shapes=[
            pltpu.VMEM(back.shape, back.dtype),
            pltpu.VMEM(fwd.shape, fwd.dtype),
            pltpu.VMEM(link.shape, link.dtype),
            pltpu.VMEM(table.shape, jnp.float32),
            pltpu.VMEM((2, 4, 3, columns, plane), jnp.bfloat16),
            pltpu.VMEM((gammas,) + table.shape[1:], jnp.float32),
            pltpu.VMEM((56, plane), jnp.float32),
            pltpu.VMEM((groups, 2, 2, 2, 3, GROUP, plane), jnp.bfloat16),
            pltpu.VMEM((groups, 2, 2, 2, 3, GROUP, plane), jnp.bfloat16),
            pltpu.VMEM((2, 4 * columns, 6 * plane), jnp.bfloat16),
            pltpu.VMEM((2, 4, 3, columns, plane), jnp.float32),
            pltpu.VMEM((groups, moments, width, 6 * plane), jnp.bfloat16),
            pltpu.VMEM((groups, moments, spaces, 4 * rows, width), jnp.float32),
            pltpu.VMEM((groups, moments, spaces, 4 * rows, width), jnp.bfloat16),
            pltpu.VMEM((groups, moments, slots, 4 * rows, width), jnp.bfloat16),
            pltpu.SemaphoreType.DMA((4,)),
            pltpu.SemaphoreType.DMA((2,)),
            pltpu.SemaphoreType.DMA((groups, 2)),
            pltpu.SemaphoreType.DMA((groups, 2)),
            pltpu.SemaphoreType.DMA((groups, moments, spaces - 1)),
            pltpu.SemaphoreType.DMA((groups, moments, slots)),
            pltpu.SemaphoreType.REGULAR,
        ],
        compiler_params=pltpu.CompilerParams(collective_id=0, has_side_effects=True),
    )(back, fwd, link, momenta, gamma_list, table)
    out = pl.pallas_call(
        store_kernel,
        out_shape=jax.ShapeDtypeStruct(out_shape, jnp.float32),
        in_specs=[vmem],
        out_specs=anywhere,
        scratch_shapes=[pltpu.SemaphoreType.DMA((moments,))],
    )(pltpu.with_memory_space_constraint(values, pltpu.VMEM))
    return out.reshape(2, moments, gammas, times, rows, columns)


def solution(mesh):
    in_specs = (
        P("parts", "tm", None, "spin", None, "space", None),
        P("parts", "tm", None, "spin", None, "space", None),
        P("parts", None, None, None, "tm", "space", None),
        P(),
        P(),
    )
    out_specs = P("parts", None, None, "tm", "space", "spin")
    return jax.shard_map(
        functools.partial(body, mesh),
        mesh=mesh,
        in_specs=in_specs,
        out_specs=out_specs,
        check_vma=False,
    )
```

time: 22.4 us -> 22.3 us (level)
  no operation moved by 1% of the time
where the time goes in v1:
time: 22.3 us; the launch traced here: 22.1 us
  Pallas kernels  22.1 us (99%)
    pallas_call x1, Pallas kernels, body(): pl.pallas_call(functools.partial(kernel, spaces, LX, full_z), out_shape=p...  21.2 us
    pallas_call x1, Pallas kernels, body(): pl.pallas_call(store_kernel, out_shape=jax.ShapeDtypeStruct(out_shape, jn...  0.9 us

profile of v1, /device:TPU:0, one launch (start us, length us, event | category | flops | bytes accessed | tf_op | source)
XLA Modules:
  0.0 22.1 jit_solution(15337817884761352768)
XLA Ops:
  0.0 21.2 %shard_map.64.value_ref = f32[2,3,16,16,32]{4,3,2,1,0:T(8,128)S(1)} custom-call(bf16[2,4,3,32,128]{4,3,2,1,0:T(8,128)(2,1)} %bitcast.18, bf16[2,4,3,32,128]{4,3,2,1,0:T(8,128)(2,1)} %bitcast.19, bf16[3,3,3,2,128]{4,3,2,1,0:T(2,128)(2,1)} %bitcast.20, s32[3,3]{1,0:T(4,128)} %momenta_ref.1, s32[16]{0:T(128)} %gamma_ref.1, f32[16,8,128]{2,1,0:T(8,128)} %constant.2.clone.table_hbm), custom_call_target="tpu_custom_call" | custom-call | tf_op jit(solution)/shard_map/pallas_call | solution.py:509
  21.2 0.9 %shard_map.65 = f32[2,3,16,16,32]{4,3,2,1,0:T(8,128)} custom-call(f32[2,3,16,16,32]{4,3,2,1,0:T(8,128)S(1)} %shard_map.64.value_ref), custom_call_target="tpu_custom_call" | custom-call | tf_op jit(solution)/shard_map/pallas_call | solution.py:540

commit v2 on v1

--- a/solution.py
+++ b/solution.py
@@ -31,6 +31,19 @@
     return singles, np.stack(basis)
 
 
+def pick_table(basis):
+    table = np.zeros((len(basis), 8), np.int32)
+    real = {1: 0, -1: 1, 1j: 3, -1j: 2}
+    imag = {1: 2, -1: 3, 1j: 0, -1j: 1}
+    for number, matrix in enumerate(basis):
+        for s in range(4):
+            (t,) = np.flatnonzero(matrix[s])
+            unit = complex(matrix[s, t])
+            table[number, s] = (real[unit] * 4 + s) * 4 + t
+            table[number, 4 + s] = (imag[unit] * 4 + s) * 4 + t
+    return table
+
+
 def unit_times(unit, value):
     real, imag = value
     if unit == 1:
@@ -68,19 +81,22 @@
     spaces,
     width_x,
     full_z,
+    scaling,
     back_hbm,
     fwd_hbm,
     link_hbm,
-    momenta_ref,
-    gamma_ref,
+    momenta_hbm,
+    gamma_hbm,
     table_hbm,
     out_ref,
     back_ref,
     fwd_ref,
     link_ref,
     table_ref,
+    momenta_ref,
+    gamma_ref,
     other_back,
-    chosen_ref,
+    folded,
     links,
     halo_send,
     halo_recv,
@@ -90,12 +106,14 @@
     pair,
     chunk_send,
     chunk_recv,
+    relay_recv,
     load_sems,
     back_sems,
-    halo_send_sems,
+    halo_send_sem,
     halo_recv_sems,
-    chunk_send_sems,
+    chunk_send_sem,
     chunk_recv_sems,
+    relay_sems,
     ready_sem,
 ):
     loads = [
@@ -106,6 +124,8 @@
                 (link_hbm, link_ref),
                 (back_hbm, back_ref),
                 (table_hbm, table_ref),
+                (momenta_hbm, momenta_ref),
+                (gamma_hbm, gamma_ref),
             )
         )
     ]
@@ -141,11 +161,11 @@
 
                 @pl.when(here == 0)
                 def _(g=g, number=number):
-                    chunk_recv[g, number, 0] = jnp.zeros_like(chunk_recv[g, number, 0])
+                    chunk_recv[number, g, 0] = jnp.zeros_like(chunk_recv[number, g, 0])
 
                 @pl.when(here == last)
                 def _(g=g, number=number):
-                    chunk_recv[g, number, last - 1] = jnp.zeros_like(chunk_recv[g, number, 0])
+                    chunk_recv[number, g, last - 1] = jnp.zeros_like(chunk_recv[number, g, 0])
 
     for load in loads[:2]:
         load.wait()
@@ -216,8 +236,8 @@
         return pltpu.make_async_remote_copy(
             src_ref=halo_send.at[g, side],
             dst_ref=halo_recv.at[g, side],
-            send_sem=halo_send_sems.at[g, side],
-            recv_sem=halo_recv_sems.at[g, side],
+            send_sem=halo_send_sem,
+            recv_sem=halo_recv_sems.at[g],
             device_id={"space": before if side == 0 else after},
         )
 
@@ -236,15 +256,11 @@
         if g == 0:
             pl.semaphore_wait(barrier, last + core)
 
-        @pl.when(here == last)
-        def _(g=g):
-            halo_copy(g, 1).start()
-            halo_copy(g, 0).start()
-
-        @pl.when(here != last)
-        def _(g=g):
-            halo_copy(g, 0).start()
-            halo_copy(g, 1).start()
+        pl.when(here != last)(halo_copy(g, 0).start)
+        pl.when(here != 0)(halo_copy(g, 1).start)
+    for g in range(groups):
+        pl.when(here == last)(halo_copy(g, 0).start)
+        pl.when(here == 0)(halo_copy(g, 1).start)
 
     loads[2].wait()
     back_copy = pltpu.make_async_remote_copy(
@@ -286,6 +302,8 @@
 
     lax.fori_loop(0, groups, plane_group, 0)
 
+    for load in loads[3:]:
+        load.wait()
     sites = lax.broadcasted_iota(jnp.int32, (8, plane), 1)
     coord_x = lax.rem(sites, width_x).astype(jnp.float32)
     coord_y = lax.div(sites, width_x).astype(jnp.float32)
@@ -299,10 +317,6 @@
         theta = (2.0 * math.pi) * (turns - jnp.floor(turns))
         phases.append((jnp.cos(theta)[:1, :], jnp.sin(theta)[:1, :]))
 
-    loads[3].wait()
-    for k in range(gammas):
-        chosen_ref[k] = table_ref[gamma_ref[k]]
-
     def arrange(owner, source):
         for part in range(2):
             for c in range(3):
@@ -324,45 +338,51 @@
     back_copy.wait_recv()
     arrange(1 - core, other_back)
 
-    def is_long(step):
-        if not relayed or step not in (1, last):
-            return None
-        return here == (last if step == 1 else 0)
-
     inner = (here != 0) & (here != last)
     far = jnp.where(here == 1, last, 0)
 
-    def chunk_copy(g, number, step):
-        target = source = lax.rem(here + step, spaces)
-        slot = step - 1
-        long = is_long(step)
-        if long is not None:
-            target = jnp.where(long, last - 1 if step == 1 else 1, target)
-            slot = jnp.where(long, last, slot)
+    def chunk_copy(g, number, step, relay=False):
+        owner = lax.rem(here + step, spaces)
+        if relay:
+            target = last - 1 if step == 1 else 1
+            target_ref, recv_sem = relay_recv.at[g, number], relay_sems.at[g, number]
+        else:
+            target = owner
+            target_ref, recv_sem = chunk_recv.at[number, g, step - 1], chunk_recv_sems.at[number]
         return pltpu.make_async_remote_copy(
-            src_ref=chunk_send.at[g, number, source],
-            dst_ref=chunk_recv.at[g, number, slot],
-            send_sem=chunk_send_sems.at[g, number, step - 1],
-            recv_sem=chunk_recv_sems.at[g, number, slot],
+            src_ref=chunk_send.at[g, number, owner],
+            dst_ref=target_ref,
+            send_sem=chunk_send_sem,
+            recv_sem=recv_sem,
             device_id={"space": target},
         )
 
-    def wait_chunk(g, number, slot):
-        pltpu.make_async_remote_copy(
-            src_ref=chunk_send.at[g, number, 0],
-            dst_ref=chunk_recv.at[g, number, slot],
-            send_sem=chunk_send_sems.at[g, number, 0],
-            recv_sem=chunk_recv_sems.at[g, number, slot],
+    def wait_all(ref, send_sem, recv_sem):
+        copy = pltpu.make_async_remote_copy(
+            src_ref=ref,
+            dst_ref=ref,
+            send_sem=send_sem,
+            recv_sem=recv_sem,
             device_id={"space": after},
-        ).wait_recv()
+        )
+        return copy
+
+    def wait_chunks(number):
+        def wait(first, end):
+            ref = chunk_recv.at[number, :, first:end]
+            wait_all(ref, chunk_send_sem, chunk_recv_sems.at[number]).wait_recv()
+
+        if not relayed:
+            wait(0, last)
+            return
+        pl.when(inner)(functools.partial(wait, 0, last))
+        pl.when(here == 0)(functools.partial(wait, 1, last))
+        pl.when(here == last)(functools.partial(wait, 0, last - 1))
 
     chunk_rows = 4 * rows
     order = sorted(range(1, spaces), key=lambda step: -min(step, spaces - step))
-    if relayed:
-        order = [last, 1] + [step for step in order if step not in (1, last)]
-    for g in range(groups):
-        for side in range(2):
-            halo_copy(g, side).wait_recv()
+    def depth_group(g):
+        wait_all(halo_recv.at[g], halo_send_sem, halo_recv_sems.at[g]).wait_recv()
         received = [
             [
                 [
@@ -380,41 +400,76 @@
         behind = received[1]
         upper = subtracted(ahead, behind)
         lower = small_times(-singles[2][2:, :2], added(ahead, behind))
+        store_weave(group(g), upper + lower, False)
+
+    def rotate(g, number, dot, top):
         cols = group(g)
-        store_weave(cols, upper + lower, False)
-        for number in range(moments):
-            cosine, sine = phases[number]
-            for s in range(4):
-                for c in range(3):
-                    real = weave[0, s, c, cols, :]
-                    imag = weave[1, s, c, cols, :]
-                    turned_real = (cosine * real + sine * imag).astype(jnp.bfloat16)
-                    turned_imag = (cosine * imag - sine * real).astype(jnp.bfloat16)
-                    rows_at = slice(s * GROUP, (s + 1) * GROUP)
-                    rows_next = slice((4 + s) * GROUP, (5 + s) * GROUP)
-                    lanes_at = slice(c * plane, (c + 1) * plane)
-                    lanes_next = slice((3 + c) * plane, (4 + c) * plane)
-                    weave_mm[g, number, rows_at, lanes_at] = turned_real
-                    weave_mm[g, number, rows_at, lanes_next] = turned_imag
-                    weave_mm[g, number, rows_next, lanes_at] = turned_imag
-                    weave_mm[g, number, rows_next, lanes_next] = -turned_real
-            product = lax.dot_general(
-                rows_scr[...].reshape(8 * columns, 6 * plane),
-                weave_mm[g, number],
-                (((1,), (1,)), ((), ())),
-                preferred_element_type=jnp.float32,
-            )
+        cosine, sine = phases[number]
+        for s in range(4):
+            for c in range(3):
+                real = weave[0, s, c, cols, :]
+                imag = weave[1, s, c, cols, :]
+                turned_real = (cosine * real + sine * imag).astype(jnp.bfloat16)
+                turned_imag = (cosine * imag - sine * real).astype(jnp.bfloat16)
+                at = top + 2 * s * GROUP
+                rows_at = slice(at, at + GROUP)
+                rows_next = slice(at + GROUP, at + 2 * GROUP)
+                lanes_at = slice(c * plane, (c + 1) * plane)
+                lanes_next = slice((3 + c) * plane, (4 + c) * plane)
+                weave_mm[dot, rows_at, lanes_at] = turned_real
+                weave_mm[dot, rows_at, lanes_next] = turned_imag
+                weave_mm[dot, rows_next, lanes_at] = turned_imag
+                weave_mm[dot, rows_next, lanes_next] = -turned_real
+
+    def send_first(g, number):
+        if not relayed:
+            for step in order:
+                chunk_copy(g, number, step).start()
+            return
+        for step in (1, last):
+            pl.when(inner)(chunk_copy(g, number, step).start)
+            end = last if step == 1 else 0
+            pl.when(here == end)(chunk_copy(g, number, step, True).start)
+
+    def send_rest(g, number, phase):
+        if phase == 0:
+            for step in range(2, last):
+                delayed = inner & (lax.rem(here + step, spaces) == far)
+                pl.when(jnp.logical_not(delayed))(chunk_copy(g, number, step).start)
+        else:
+            for step in (1, last):
+                first = inner | (here == (last if step == 1 else 0))
+                pl.when(jnp.logical_not(first))(chunk_copy(g, number, step).start)
+
+    width = pair.shape[-1]
+    pieces = [(g, number) for g in range(groups) for number in range(moments)]
+    ready = 0
+    for dot in range((len(pieces) + 1) // 2):
+        inside = pieces[2 * dot : 2 * dot + 2]
+        while ready <= inside[-1][0]:
+            depth_group(ready)
+            ready += 1
+        for index, (g, number) in enumerate(inside):
+            rotate(g, number, dot, index * width)
+        product = lax.dot_general(
+            rows_scr[...].reshape(8 * columns, 6 * plane),
+            weave_mm[dot, : len(inside) * width],
+            (((1,), (1,)), ((), ())),
+            preferred_element_type=jnp.float32,
+        )
+        for index, (g, number) in enumerate(inside):
             for target in range(spaces):
-                piece = product[target * chunk_rows : (target + 1) * chunk_rows]
+                piece = product[
+                    target * chunk_rows : (target + 1) * chunk_rows,
+                    index * width : (index + 1) * width,
+                ]
                 pair[g, number, target] = piece
                 chunk_send[g, number, target] = piece.astype(jnp.bfloat16)
-            for step in order:
-                copy = chunk_copy(g, number, step)
-                if relayed and 1 < step < last:
-                    delayed = inner & (lax.rem(here + step, spaces) == far)
-                    pl.when(jnp.logical_not(delayed))(copy.start)
-                else:
-                    copy.start()
+            send_first(g, number)
+    if relayed:
+        for phase in range(2):
+            for g, number in pieces:
+                send_rest(g, number, phase)
 
     if relayed:
         for g in range(groups):
@@ -423,50 +478,50 @@
 
                     @pl.when(((here == 1) & (step == last - 1)) | ((here == last - 1) & (step == 2)))
                     def _(g=g, number=number, step=step):
-                        wait_chunk(g, number, last)
+                        chunk_copy(g, number, last, True).wait_recv()
                         target = lax.rem(here + step, spaces)
-                        summed = pair[g, number, target] + chunk_recv[g, number, last].astype(
+                        summed = pair[g, number, target] + relay_recv[g, number].astype(
                             jnp.float32
                         )
                         chunk_send[g, number, target] = summed.astype(jnp.bfloat16)
                         chunk_copy(g, number, step).start()
 
-    width = pair.shape[-1]
-    half = width // 2
-    for g in range(groups):
-        for number in range(moments):
-            total = pair[g, number, here]
-            for step in range(1, spaces):
-                if relayed and step in (1, last):
-                    end = 0 if step == 1 else last
-                    pl.when(here != end)(
-                        functools.partial(wait_chunk, g, number, step - 1)
-                    )
-                else:
-                    wait_chunk(g, number, step - 1)
-                total = total + chunk_recv[g, number, step - 1].astype(jnp.float32)
-            values = [total[s * rows : (s + 1) * rows] for s in range(4)]
-            turned = [pltpu.roll(value, half, 1) for value in values]
-            for k in range(gammas):
-                summed = None
-                for s in range(4):
-                    term = chosen_ref[k, s : s + 1, :] * values[s]
-                    term = term + chosen_ref[k, 4 + s : 5 + s, :] * turned[s]
-                    summed = term if summed is None else summed + term
-                summed = summed + pltpu.roll(summed, width - GROUP, 1)
-                summed = summed + pltpu.roll(summed, width - 2 * GROUP, 1)
-                for part in range(2):
-                    out_ref[part, number, k, :, g * GROUP : (g + 1) * GROUP] = summed[
-                        :, part * half : part * half + GROUP
-                    ]
-
-    back_copy.wait_send()
-    for g in range(groups):
-        for side in range(2):
-            halo_copy(g, side).wait_send()
-        for number in range(moments):
-            for step in range(1, spaces):
-                chunk_copy(g, number, step).wait_send()
+    def summed_piece(g, number):
+        total = pair[g, number, here]
+        for step in range(1, spaces):
+            total = total + chunk_recv[number, g, step - 1].astype(jnp.float32)
+        return total * scaling
+
+    lane = lax.broadcasted_iota(jnp.int32, (rows, width), 1)
+    slot = lax.div(lax.rem(lane, groups * GROUP), GROUP)
+    for number in range(moments):
+        if number == moments - 1:
+            back_copy.wait_send()
+            wait_all(halo_send, halo_send_sem, halo_recv_sems.at[0]).wait_send()
+            sent = chunk_send.at[:, :, :last]
+            wait_all(sent, chunk_send_sem, chunk_recv_sems.at[0]).wait_send()
+        wait_chunks(number)
+        totals = [summed_piece(g, number) for g in range(groups)]
+        for s in range(4):
+            for part in range(2):
+                merged = None
+                for g in range(groups):
+                    value = totals[g][s * rows : (s + 1) * rows]
+                    if g != part:
+                        value = pltpu.roll(value, (width + (g - part) * GROUP) % width, 1)
+                    merged = value if merged is None else jnp.where(slot == g, value, merged)
+                for t in range(4):
+                    value = merged
+                    if t:
+                        value = pltpu.roll(merged, width - t * 2 * GROUP, 1)
+                    folded[(2 * part * 4 + s) * 4 + t, number] = value
+                    folded[((2 * part + 1) * 4 + s) * 4 + t, number] = -value
+        for k in range(gammas):
+            for part in range(2):
+                picks = [table_ref[gamma_ref[k], part * 4 + s] for s in range(4)]
+                value = folded[picks[0], number] + folded[picks[1], number]
+                value = value + (folded[picks[2], number] + folded[picks[3], number])
+                out_ref[part, number, k] = value[:, :columns]
 
 
 def store_kernel(value_ref, out_hbm, sems):
@@ -496,43 +551,42 @@
     full_z = layers * spaces
     scaling = 0.5 / math.sqrt(3.0 * plane * full_z)
     _, basis = gamma_tables()
-    plain = np.concatenate([basis.real, basis.real], axis=2)
-    crossed = np.concatenate([-basis.imag, basis.imag], axis=2)
-    table = np.concatenate([plain, crossed], axis=1)
-    table = (np.repeat(table, GROUP, axis=2) * scaling).astype(np.float32)
-    width = table.shape[2]
-    slots = spaces if 4 <= spaces <= LINE else spaces - 1
+    table = pick_table(basis)
+    width = 8 * GROUP
     vmem = pl.BlockSpec(memory_space=pltpu.VMEM)
     anywhere = pl.BlockSpec(memory_space=pl.ANY)
-    smem = pl.BlockSpec(memory_space=pltpu.SMEM)
     out_shape = (2, moments, gammas, rows, columns)
     values = pl.pallas_call(
-        functools.partial(kernel, spaces, LX, full_z),
+        functools.partial(kernel, spaces, LX, full_z, scaling),
         out_shape=pltpu.VMEM(out_shape, jnp.float32),
-        in_specs=[anywhere, anywhere, anywhere, smem, smem, anywhere],
+        in_specs=[anywhere] * 6,
         out_specs=vmem,
         scratch_shapes=[
             pltpu.VMEM(back.shape, back.dtype),
             pltpu.VMEM(fwd.shape, fwd.dtype),
             pltpu.VMEM(link.shape, link.dtype),
-            pltpu.VMEM(table.shape, jnp.float32),
+            pltpu.SMEM(table.shape, table.dtype),
+            pltpu.SMEM(momenta.shape, momenta.dtype),
+            pltpu.SMEM(gamma_list.shape, gamma_list.dtype),
             pltpu.VMEM((2, 4, 3, columns, plane), jnp.bfloat16),
-            pltpu.VMEM((gammas,) + table.shape[1:], jnp.float32),
+            pltpu.VMEM((64, moments, rows, width), jnp.float32),
             pltpu.VMEM((56, plane), jnp.float32),
             pltpu.VMEM((groups, 2, 2, 2, 3, GROUP, plane), jnp.bfloat16),
             pltpu.VMEM((groups, 2, 2, 2, 3, GROUP, plane), jnp.bfloat16),
             pltpu.VMEM((2, 4 * columns, 6 * plane), jnp.bfloat16),
             pltpu.VMEM((2, 4, 3, columns, plane), jnp.float32),
-            pltpu.VMEM((groups, moments, width, 6 * plane), jnp.bfloat16),
+            pltpu.VMEM(((groups * moments + 1) // 2, 2 * width, 6 * plane), jnp.bfloat16),
             pltpu.VMEM((groups, moments, spaces, 4 * rows, width), jnp.float32),
             pltpu.VMEM((groups, moments, spaces, 4 * rows, width), jnp.bfloat16),
-            pltpu.VMEM((groups, moments, slots, 4 * rows, width), jnp.bfloat16),
-            pltpu.SemaphoreType.DMA((4,)),
+            pltpu.VMEM((moments, groups, spaces - 1, 4 * rows, width), jnp.bfloat16),
+            pltpu.VMEM((groups, moments, 4 * rows, width), jnp.bfloat16),
+            pltpu.SemaphoreType.DMA((6,)),
             pltpu.SemaphoreType.DMA((2,)),
-            pltpu.SemaphoreType.DMA((groups, 2)),
-            pltpu.SemaphoreType.DMA((groups, 2)),
-            pltpu.SemaphoreType.DMA((groups, moments, spaces - 1)),
-            pltpu.SemaphoreType.DMA((groups, moments, slots)),
+            pltpu.SemaphoreType.DMA,
+            pltpu.SemaphoreType.DMA((groups,)),
+            pltpu.SemaphoreType.DMA,
+            pltpu.SemaphoreType.DMA((moments,)),
+            pltpu.SemaphoreType.DMA((groups, moments)),
             pltpu.SemaphoreType.REGULAR,
         ],
         compiler_params=pltpu.CompilerParams(collective_id=0, has_side_effects=True),

time: 22.3 us -> 19.9 us (0.89)
  Pallas kernels: 22.1 us -> 19.8 us
    pallas_call x1, Pallas kernels: 21.2 us -> 18.9 us  [body(): pl.pallas_call(functools.partial(kernel, spaces, LX, full_z, scaling), ou...]
where the time goes in v2:
time: 19.9 us; the launch traced here: 19.8 us
  Pallas kernels  19.8 us (99%)
    pallas_call x1, Pallas kernels, body(): pl.pallas_call(functools.partial(kernel, spaces, LX, full_z, scaling), ou...  18.9 us
    pallas_call x1, Pallas kernels, body(): pl.pallas_call(store_kernel, out_shape=jax.ShapeDtypeStruct(out_shape, jn...  0.9 us

profile of v2, /device:TPU:0, one launch (start us, length us, event | category | flops | bytes accessed | tf_op | source)
XLA Modules:
  0.0 19.8 jit_solution(4600294922404834181)
XLA Ops:
  0.0 18.9 %shard_map.64.value_ref = f32[2,3,16,16,32]{4,3,2,1,0:T(8,128)S(1)} custom-call(bf16[2,4,3,32,128]{4,3,2,1,0:T(8,128)(2,1)} %bitcast.18, bf16[2,4,3,32,128]{4,3,2,1,0:T(8,128)(2,1)} %bitcast.19, bf16[3,3,3,2,128]{4,3,2,1,0:T(2,128)(2,1)} %bitcast.20, s32[3,3]{1,0:T(4,128)} %momenta_hbm.1, s32[16]{0:T(128)} %gamma_hbm.1, s32[16,8]{1,0:T(8,128)} %constant.2.clone.table_hbm), custom_call_target="tpu_custom_call" | custom-call | tf_op jit(solution)/shard_map/pallas_call | solution.py:559
  18.9 0.9 %shard_map.65 = f32[2,3,16,16,32]{4,3,2,1,0:T(8,128)} custom-call(f32[2,3,16,16,32]{4,3,2,1,0:T(8,128)S(1)} %shard_map.64.value_ref), custom_call_target="tpu_custom_call" | custom-call | tf_op jit(solution)/shard_map/pallas_call | solution.py:594

commit v3 on v2

--- a/solution.py
+++ b/solution.py
@@ -31,17 +31,18 @@
     return singles, np.stack(basis)
 
 
-def pick_table(basis):
-    table = np.zeros((len(basis), 8), np.int32)
-    real = {1: 0, -1: 1, 1j: 3, -1j: 2}
-    imag = {1: 2, -1: 3, 1j: 0, -1j: 1}
-    for number, matrix in enumerate(basis):
-        for s in range(4):
-            (t,) = np.flatnonzero(matrix[s])
-            unit = complex(matrix[s, t])
-            table[number, s] = (real[unit] * 4 + s) * 4 + t
-            table[number, 4 + s] = (imag[unit] * 4 + s) * 4 + t
-    return table
+def picked(units, part):
+    if all(unit.imag == 0 for unit in units):
+        return part, [int(unit.real) for unit in units]
+    assert all(unit.real == 0 for unit in units)
+    sign = -1 if part == 0 else 1
+    return 1 - part, [sign * int(unit.imag) for unit in units]
+
+
+def signed_sum(first_sign, first, second_sign, second):
+    if first_sign > 0:
+        return first + second if second_sign > 0 else first - second
+    return second - first if second_sign > 0 else -first - second
 
 
 def unit_times(unit, value):
@@ -87,16 +88,14 @@
     link_hbm,
     momenta_hbm,
     gamma_hbm,
-    table_hbm,
     out_ref,
     back_ref,
     fwd_ref,
     link_ref,
-    table_ref,
     momenta_ref,
     gamma_ref,
     other_back,
-    folded,
+    results,
     links,
     halo_send,
     halo_recv,
@@ -105,6 +104,7 @@
     weave_mm,
     pair,
     chunk_send,
+    far_send,
     chunk_recv,
     relay_recv,
     load_sems,
@@ -115,6 +115,7 @@
     chunk_recv_sems,
     relay_sems,
     ready_sem,
+    turn_sem,
 ):
     loads = [
         pltpu.make_async_copy(source, target, load_sems.at[number])
@@ -123,7 +124,6 @@
                 (fwd_hbm, fwd_ref),
                 (link_hbm, link_ref),
                 (back_hbm, back_ref),
-                (table_hbm, table_ref),
                 (momenta_hbm, momenta_ref),
                 (gamma_hbm, gamma_ref),
             )
@@ -143,13 +143,18 @@
     core = lax.axis_index("spin")
     after = lax.rem(here + 1, spaces)
     before = lax.rem(here + last, spaces)
-    singles, _ = gamma_tables()
+    singles, basis = gamma_tables()
 
     barrier = pltpu.get_barrier_semaphore()
-    for step in range(1, spaces):
-        pl.semaphore_signal(
-            barrier, inc=1, device_id={"space": lax.rem(here + step, spaces)}
-        )
+    if relayed:
+        greeted = 2
+        for target in (before, after):
+            pl.semaphore_signal(barrier, inc=1, device_id={"space": target})
+    else:
+        greeted = last
+        for step in range(1, spaces):
+            target = lax.rem(here + step, spaces)
+            pl.semaphore_signal(barrier, inc=1, device_id={"space": target})
 
     @pl.when(core == 0)
     def _():
@@ -254,7 +259,7 @@
                             jnp.bfloat16
                         )
         if g == 0:
-            pl.semaphore_wait(barrier, last + core)
+            pl.semaphore_wait(barrier, greeted + core)
 
         pl.when(here != last)(halo_copy(g, 0).start)
         pl.when(here != 0)(halo_copy(g, 1).start)
@@ -339,18 +344,20 @@
     arrange(1 - core, other_back)
 
     inner = (here != 0) & (here != last)
-    far = jnp.where(here == 1, last, 0)
+    far = jnp.where(2 * here < spaces, last, 0)
 
     def chunk_copy(g, number, step, relay=False):
         owner = lax.rem(here + step, spaces)
+        source_ref = chunk_send.at[g, number, owner]
         if relay:
+            source_ref = far_send.at[g, number]
             target = last - 1 if step == 1 else 1
             target_ref, recv_sem = relay_recv.at[g, number], relay_sems.at[g, number]
         else:
             target = owner
             target_ref, recv_sem = chunk_recv.at[number, g, step - 1], chunk_recv_sems.at[number]
         return pltpu.make_async_remote_copy(
-            src_ref=chunk_send.at[g, number, owner],
+            src_ref=source_ref,
             dst_ref=target_ref,
             send_sem=chunk_send_sem,
             recv_sem=recv_sem,
@@ -421,6 +428,10 @@
                 weave_mm[dot, rows_next, lanes_at] = turned_imag
                 weave_mm[dot, rows_next, lanes_next] = -turned_real
 
+    def send_far(g, number):
+        pl.when(here == last)(chunk_copy(g, number, 1, True).start)
+        pl.when(here == 0)(chunk_copy(g, number, last, True).start)
+
     def send_first(g, number):
         if not relayed:
             for step in order:
@@ -428,48 +439,67 @@
             return
         for step in (1, last):
             pl.when(inner)(chunk_copy(g, number, step).start)
-            end = last if step == 1 else 0
-            pl.when(here == end)(chunk_copy(g, number, step, True).start)
-
-    def send_rest(g, number, phase):
-        if phase == 0:
-            for step in range(2, last):
-                delayed = inner & (lax.rem(here + step, spaces) == far)
-                pl.when(jnp.logical_not(delayed))(chunk_copy(g, number, step).start)
-        else:
-            for step in (1, last):
-                first = inner | (here == (last if step == 1 else 0))
-                pl.when(jnp.logical_not(first))(chunk_copy(g, number, step).start)
+
+    def send_rest(those):
+        for step in range(2, last):
+            delayed = inner & (lax.rem(here + step, spaces) == far)
+            for g in those:
+                for number in range(moments):
+                    pl.when(jnp.logical_not(delayed))(chunk_copy(g, number, step).start)
+        for step in (1, last):
+            near = here == (0 if step == 1 else last)
+            for g in those:
+                for number in range(moments):
+                    pl.when(near)(chunk_copy(g, number, step).start)
 
     width = pair.shape[-1]
-    pieces = [(g, number) for g in range(groups) for number in range(moments)]
-    ready = 0
-    for dot in range((len(pieces) + 1) // 2):
-        inside = pieces[2 * dot : 2 * dot + 2]
-        while ready <= inside[-1][0]:
-            depth_group(ready)
-            ready += 1
-        for index, (g, number) in enumerate(inside):
-            rotate(g, number, dot, index * width)
-        product = lax.dot_general(
-            rows_scr[...].reshape(8 * columns, 6 * plane),
-            weave_mm[dot, : len(inside) * width],
-            (((1,), (1,)), ((), ())),
-            preferred_element_type=jnp.float32,
+
+    def product(g, rows_in):
+        return lax.dot_general(
+            rows_in, weave_mm[g], (((1,), (1,)), ((), ())), preferred_element_type=jnp.float32
         )
-        for index, (g, number) in enumerate(inside):
-            for target in range(spaces):
-                piece = product[
-                    target * chunk_rows : (target + 1) * chunk_rows,
-                    index * width : (index + 1) * width,
+
+    far_owner = lax.div(far * rows, columns)
+    far_row = pl.multiple_of(lax.rem(far * 4 * rows, 4 * columns), chunk_rows)
+    for g in range(groups):
+        depth_group(g)
+        for number in range(moments):
+            rotate(g, number, g, number * width)
+        if relayed:
+            value = product(g, rows_scr[far_owner, pl.ds(far_row, chunk_rows), :])
+            for number in range(moments):
+                piece = value[:, number * width : (number + 1) * width]
+                far_send[g, number] = piece.astype(jnp.bfloat16)
+                send_far(g, number)
+            if g == groups - 1:
+
+                @pl.when((core == 0) & jnp.logical_not(inner))
+                def _():
+                    pl.semaphore_signal(turn_sem, inc=1, device_id={"spin": 1 - core})
+
+        value = product(g, rows_scr[...].reshape(8 * columns, 6 * plane))
+        for number in range(moments):
+            for owner in range(spaces):
+                piece = value[
+                    owner * chunk_rows : (owner + 1) * chunk_rows,
+                    number * width : (number + 1) * width,
                 ]
-                pair[g, number, target] = piece
-                chunk_send[g, number, target] = piece.astype(jnp.bfloat16)
+                pair[g, number, owner] = piece
+                chunk_send[g, number, owner] = piece.astype(jnp.bfloat16)
             send_first(g, number)
+        if relayed and g < groups - 1:
+            pl.when((core == 1) & jnp.logical_not(inner))(
+                functools.partial(send_rest, range(g, g + 1))
+            )
     if relayed:
-        for phase in range(2):
-            for g, number in pieces:
-                send_rest(g, number, phase)
+        @pl.when((core == 1) & jnp.logical_not(inner))
+        def _():
+            pl.semaphore_wait(turn_sem, 1)
+            send_rest(range(groups - 1, groups))
+
+        @pl.when((core == 0) | inner)
+        def _():
+            send_rest(range(groups))
 
     if relayed:
         for g in range(groups):
@@ -494,34 +524,57 @@
 
     lane = lax.broadcasted_iota(jnp.int32, (rows, width), 1)
     slot = lax.div(lax.rem(lane, groups * GROUP), GROUP)
+    back_copy.wait_send()
+    wait_all(halo_send, halo_send_sem, halo_recv_sems.at[0]).wait_send()
+    wait_all(chunk_send.at[:, :, :last], chunk_send_sem, chunk_recv_sems.at[0]).wait_send()
     for number in range(moments):
-        if number == moments - 1:
-            back_copy.wait_send()
-            wait_all(halo_send, halo_send_sem, halo_recv_sems.at[0]).wait_send()
-            sent = chunk_send.at[:, :, :last]
-            wait_all(sent, chunk_send_sem, chunk_recv_sems.at[0]).wait_send()
-        wait_chunks(number)
+        if number == 0:
+            wait_chunks(0)
+        elif number == 1:
+            for other in range(1, moments):
+                wait_chunks(other)
         totals = [summed_piece(g, number) for g in range(groups)]
-        for s in range(4):
-            for part in range(2):
+        parts = []
+        for part in range(2):
+            merged_rows = []
+            for s in range(4):
                 merged = None
                 for g in range(groups):
                     value = totals[g][s * rows : (s + 1) * rows]
                     if g != part:
                         value = pltpu.roll(value, (width + (g - part) * GROUP) % width, 1)
                     merged = value if merged is None else jnp.where(slot == g, value, merged)
-                for t in range(4):
-                    value = merged
-                    if t:
-                        value = pltpu.roll(merged, width - t * 2 * GROUP, 1)
-                    folded[(2 * part * 4 + s) * 4 + t, number] = value
-                    folded[((2 * part + 1) * 4 + s) * 4 + t, number] = -value
+                merged_rows.append(merged)
+            parts.append(merged_rows)
+        for offset in range(4):
+            sums = []
+            for part in range(2):
+                terms = []
+                for s in range(4):
+                    t = s ^ offset
+                    value = parts[part][s]
+                    terms.append(pltpu.roll(value, width - t * 2 * GROUP, 1) if t else value)
+                sums.append(
+                    {
+                        (pair_at, sign): terms[pair_at] + terms[pair_at + 1]
+                        if sign > 0
+                        else terms[pair_at] - terms[pair_at + 1]
+                        for pair_at in (0, 2)
+                        for sign in (1, -1)
+                    }
+                )
+            for index in range(len(basis)):
+                if np.flatnonzero(basis[index][0])[0] != offset:
+                    continue
+                units = [complex(basis[index][s, s ^ offset]) for s in range(4)]
+                for part in range(2):
+                    source, signs = picked(units, part)
+                    first = sums[source][0, signs[0] * signs[1]]
+                    second = sums[source][2, signs[2] * signs[3]]
+                    results[number, index, part] = signed_sum(signs[0], first, signs[2], second)
         for k in range(gammas):
             for part in range(2):
-                picks = [table_ref[gamma_ref[k], part * 4 + s] for s in range(4)]
-                value = folded[picks[0], number] + folded[picks[1], number]
-                value = value + (folded[picks[2], number] + folded[picks[3], number])
-                out_ref[part, number, k] = value[:, :columns]
+                out_ref[part, number, k] = results[number, gamma_ref[k], part][:, :columns]
 
 
 def store_kernel(value_ref, out_hbm, sems):
@@ -550,8 +603,6 @@
     link = jnp.transpose(gauge_links, (1, 2, 3, 4, 5, 0, 6)).reshape(3, 3, 3, 2, plane)
     full_z = layers * spaces
     scaling = 0.5 / math.sqrt(3.0 * plane * full_z)
-    _, basis = gamma_tables()
-    table = pick_table(basis)
     width = 8 * GROUP
     vmem = pl.BlockSpec(memory_space=pltpu.VMEM)
     anywhere = pl.BlockSpec(memory_space=pl.ANY)
@@ -559,28 +610,28 @@
     values = pl.pallas_call(
         functools.partial(kernel, spaces, LX, full_z, scaling),
         out_shape=pltpu.VMEM(out_shape, jnp.float32),
-        in_specs=[anywhere] * 6,
+        in_specs=[anywhere] * 5,
         out_specs=vmem,
         scratch_shapes=[
             pltpu.VMEM(back.shape, back.dtype),
             pltpu.VMEM(fwd.shape, fwd.dtype),
             pltpu.VMEM(link.shape, link.dtype),
-            pltpu.SMEM(table.shape, table.dtype),
             pltpu.SMEM(momenta.shape, momenta.dtype),
             pltpu.SMEM(gamma_list.shape, gamma_list.dtype),
             pltpu.VMEM((2, 4, 3, columns, plane), jnp.bfloat16),
-            pltpu.VMEM((64, moments, rows, width), jnp.float32),
+            pltpu.VMEM((moments, 16, 2, rows, width), jnp.float32),
             pltpu.VMEM((56, plane), jnp.float32),
             pltpu.VMEM((groups, 2, 2, 2, 3, GROUP, plane), jnp.bfloat16),
             pltpu.VMEM((groups, 2, 2, 2, 3, GROUP, plane), jnp.bfloat16),
             pltpu.VMEM((2, 4 * columns, 6 * plane), jnp.bfloat16),
             pltpu.VMEM((2, 4, 3, columns, plane), jnp.float32),
-            pltpu.VMEM(((groups * moments + 1) // 2, 2 * width, 6 * plane), jnp.bfloat16),
+            pltpu.VMEM((groups, moments * width, 6 * plane), jnp.bfloat16),
             pltpu.VMEM((groups, moments, spaces, 4 * rows, width), jnp.float32),
             pltpu.VMEM((groups, moments, spaces, 4 * rows, width), jnp.bfloat16),
+            pltpu.VMEM((groups, moments, 4 * rows, width), jnp.bfloat16),
             pltpu.VMEM((moments, groups, spaces - 1, 4 * rows, width), jnp.bfloat16),
             pltpu.VMEM((groups, moments, 4 * rows, width), jnp.bfloat16),
-            pltpu.SemaphoreType.DMA((6,)),
+            pltpu.SemaphoreType.DMA((5,)),
             pltpu.SemaphoreType.DMA((2,)),
             pltpu.SemaphoreType.DMA,
             pltpu.SemaphoreType.DMA((groups,)),
@@ -588,9 +639,10 @@
             pltpu.SemaphoreType.DMA((moments,)),
             pltpu.SemaphoreType.DMA((groups, moments)),
             pltpu.SemaphoreType.REGULAR,
+            pltpu.SemaphoreType.REGULAR,
         ],
         compiler_params=pltpu.CompilerParams(collective_id=0, has_side_effects=True),
-    )(back, fwd, link, momenta, gamma_list, table)
+    )(back, fwd, link, momenta, gamma_list)
     out = pl.pallas_call(
         store_kernel,
         out_shape=jax.ShapeDtypeStruct(out_shape, jnp.float32),

time: 19.9 us -> 19.4 us (0.975)
  Pallas kernels: 19.8 us -> 19.2 us
    pallas_call x1, Pallas kernels: 18.9 us -> 18.3 us  [body(): pl.pallas_call(functools.partial(kernel, spaces, LX, full_z, scaling), ou...]
where the time goes in v3:
time: 19.4 us; the launch traced here: 19.2 us
  Pallas kernels  19.2 us (99%)
    pallas_call x1, Pallas kernels, body(): pl.pallas_call(functools.partial(kernel, spaces, LX, full_z, scaling), ou...  18.3 us
    pallas_call x1, Pallas kernels, body(): pl.pallas_call(store_kernel, out_shape=jax.ShapeDtypeStruct(out_shape, jn...  0.9 us

profile of v3, /device:TPU:0, one launch (start us, length us, event | category | flops | bytes accessed | tf_op | source)
XLA Modules:
  0.0 19.2 jit_solution(3532597143801642275)
XLA Ops:
  0.0 18.3 %shard_map.55.value_ref = f32[2,3,16,16,32]{4,3,2,1,0:T(8,128)S(1)} custom-call(bf16[2,4,3,32,128]{4,3,2,1,0:T(8,128)(2,1)} %bitcast.18, bf16[2,4,3,32,128]{4,3,2,1,0:T(8,128)(2,1)} %bitcast.19, bf16[3,3,3,2,128]{4,3,2,1,0:T(2,128)(2,1)} %bitcast.20, s32[3,3]{1,0:T(4,128)} %momenta_hbm.1, s32[16]{0:T(128)} %gamma_hbm.1), custom_call_target="tpu_custom_call" | custom-call | tf_op jit(solution)/shard_map/pallas_call | solution.py:610
  18.3 0.9 %shard_map.56 = f32[2,3,16,16,32]{4,3,2,1,0:T(8,128)} custom-call(f32[2,3,16,16,32]{4,3,2,1,0:T(8,128)S(1)} %shard_map.55.value_ref), custom_call_target="tpu_custom_call" | custom-call | tf_op jit(solution)/shard_map/pallas_call | solution.py:646

commit v4 on v3

--- a/solution.py
+++ b/solution.py
@@ -116,6 +116,7 @@
     relay_sems,
     ready_sem,
     turn_sem,
+    near_sem,
 ):
     loads = [
         pltpu.make_async_copy(source, target, load_sems.at[number])
@@ -265,7 +266,10 @@
         pl.when(here != 0)(halo_copy(g, 1).start)
     for g in range(groups):
         pl.when(here == last)(halo_copy(g, 0).start)
-        pl.when(here == 0)(halo_copy(g, 1).start)
+        if relayed:
+            pl.when((here == 0) & (core == 0))(halo_copy(g, 1).start)
+        else:
+            pl.when(here == 0)(halo_copy(g, 1).start)
 
     loads[2].wait()
     back_copy = pltpu.make_async_remote_copy(
@@ -339,6 +343,17 @@
     def _():
         pl.semaphore_wait(ready_sem, 1)
         back_copy.start()
+
+    if relayed:
+        @pl.when((here == 0) & (core == 0))
+        def _():
+            pl.semaphore_signal(near_sem, inc=1, device_id={"spin": 1 - core})
+
+        @pl.when((here == 0) & (core == 1))
+        def _():
+            pl.semaphore_wait(near_sem, 1)
+            for g in range(groups):
+                halo_copy(g, 1).start()
 
     back_copy.wait_recv()
     arrange(1 - core, other_back)
@@ -461,22 +476,14 @@
 
     far_owner = lax.div(far * rows, columns)
     far_row = pl.multiple_of(lax.rem(far * 4 * rows, 4 * columns), chunk_rows)
-    for g in range(groups):
-        depth_group(g)
+    def far_product(g):
+        value = product(g, rows_scr[far_owner, pl.ds(far_row, chunk_rows), :])
         for number in range(moments):
-            rotate(g, number, g, number * width)
-        if relayed:
-            value = product(g, rows_scr[far_owner, pl.ds(far_row, chunk_rows), :])
-            for number in range(moments):
-                piece = value[:, number * width : (number + 1) * width]
-                far_send[g, number] = piece.astype(jnp.bfloat16)
-                send_far(g, number)
-            if g == groups - 1:
-
-                @pl.when((core == 0) & jnp.logical_not(inner))
-                def _():
-                    pl.semaphore_signal(turn_sem, inc=1, device_id={"spin": 1 - core})
-
+            piece = value[:, number * width : (number + 1) * width]
+            far_send[g, number] = piece.astype(jnp.bfloat16)
+            send_far(g, number)
+
+    def full_product(g):
         value = product(g, rows_scr[...].reshape(8 * columns, 6 * plane))
         for number in range(moments):
             for owner in range(spaces):
@@ -487,10 +494,25 @@
                 pair[g, number, owner] = piece
                 chunk_send[g, number, owner] = piece.astype(jnp.bfloat16)
             send_first(g, number)
-        if relayed and g < groups - 1:
-            pl.when((core == 1) & jnp.logical_not(inner))(
-                functools.partial(send_rest, range(g, g + 1))
-            )
+
+    for g in range(groups):
+        depth_group(g)
+        for number in range(moments):
+            rotate(g, number, g, number * width)
+        if relayed:
+            pl.when(jnp.logical_not(inner))(functools.partial(far_product, g))
+            pl.when(inner)(functools.partial(full_product, g))
+        else:
+            full_product(g)
+    if relayed:
+
+        @pl.when(jnp.logical_not(inner))
+        def _():
+            for g in range(groups):
+                full_product(g)
+                if g < groups - 1:
+                    pl.when(core == 1)(functools.partial(send_rest, range(g, g + 1)))
+
     if relayed:
         @pl.when((core == 1) & jnp.logical_not(inner))
         def _():
@@ -527,6 +549,12 @@
     back_copy.wait_send()
     wait_all(halo_send, halo_send_sem, halo_recv_sems.at[0]).wait_send()
     wait_all(chunk_send.at[:, :, :last], chunk_send_sem, chunk_recv_sems.at[0]).wait_send()
+    if relayed:
+
+        @pl.when((core == 0) & jnp.logical_not(inner))
+        def _():
+            pl.semaphore_signal(turn_sem, inc=1, device_id={"spin": 1 - core})
+
     for number in range(moments):
         if number == 0:
             wait_chunks(0)
@@ -640,6 +668,7 @@
             pltpu.SemaphoreType.DMA((groups, moments)),
             pltpu.SemaphoreType.REGULAR,
             pltpu.SemaphoreType.REGULAR,
+            pltpu.SemaphoreType.REGULAR,
         ],
         compiler_params=pltpu.CompilerParams(collective_id=0, has_side_effects=True),
     )(back, fwd, link, momenta, gamma_list)

time: 19.4 us -> 18.9 us (0.974)
  Pallas kernels: 19.2 us -> 18.8 us
    pallas_call x1, Pallas kernels: 18.3 us -> 17.9 us  [body(): pl.pallas_call(functools.partial(kernel, spaces, LX, full_z, scaling), ou...]
where the time goes in v4:
time: 18.9 us; the launch traced here: 18.8 us
  Pallas kernels  18.8 us (99%)
    pallas_call x1, Pallas kernels, body(): pl.pallas_call(functools.partial(kernel, spaces, LX, full_z, scaling), ou...  17.9 us
    pallas_call x1, Pallas kernels, body(): pl.pallas_call(store_kernel, out_shape=jax.ShapeDtypeStruct(out_shape, jn...  0.9 us

profile of v4, /device:TPU:0, one launch (start us, length us, event | category | flops | bytes accessed | tf_op | source)
XLA Modules:
  0.0 18.8 jit_solution(17562276403813161043)
XLA Ops:
  0.0 17.9 %shard_map.55.value_ref = f32[2,3,16,16,32]{4,3,2,1,0:T(8,128)S(1)} custom-call(bf16[2,4,3,32,128]{4,3,2,1,0:T(8,128)(2,1)} %bitcast.18, bf16[2,4,3,32,128]{4,3,2,1,0:T(8,128)(2,1)} %bitcast.19, bf16[3,3,3,2,128]{4,3,2,1,0:T(2,128)(2,1)} %bitcast.20, s32[3,3]{1,0:T(4,128)} %momenta_hbm.1, s32[16]{0:T(128)} %gamma_hbm.1), custom_call_target="tpu_custom_call" | custom-call | tf_op jit(solution)/shard_map/pallas_call | solution.py:638
  17.9 0.9 %shard_map.56 = f32[2,3,16,16,32]{4,3,2,1,0:T(8,128)} custom-call(f32[2,3,16,16,32]{4,3,2,1,0:T(8,128)S(1)} %shard_map.55.value_ref), custom_call_target="tpu_custom_call" | custom-call | tf_op jit(solution)/shard_map/pallas_call | solution.py:675

commit v5 on v4

--- a/solution.py
+++ b/solution.py
@@ -115,8 +115,6 @@
     chunk_recv_sems,
     relay_sems,
     ready_sem,
-    turn_sem,
-    near_sem,
 ):
     loads = [
         pltpu.make_async_copy(source, target, load_sems.at[number])
@@ -135,6 +133,7 @@
     columns = fwd_ref.shape[3]
     plane = fwd_ref.shape[4]
     moments = momenta_ref.shape[0]
+    width = pair.shape[-1]
     gammas = gamma_ref.shape[0]
     groups = columns // GROUP
     rows = columns * 2 // spaces
@@ -285,14 +284,11 @@
         pl.semaphore_signal(ready_sem, inc=1, device_id={"spin": 1 - core})
         back_copy.start()
 
-    def store_weave(cols, full, first):
+    def store_weave(cols, full):
         for s in range(4):
             for c in range(3):
                 for part in range(2):
-                    value = full[s][c][part]
-                    if not first:
-                        value = value + weave[part, s, c, cols, :]
-                    weave[part, s, c, cols, :] = value
+                    weave[part, s, c, cols, :] = full[s][c][part]
 
     def plane_group(index, carry):
         cols = group(index)
@@ -306,7 +302,7 @@
             low = small_times(-singles[mu][2:, :2], added(ahead, behind))
             upper = up if upper is None else added(upper, up)
             lower = low if lower is None else added(lower, low)
-        store_weave(cols, upper + lower, True)
+        store_weave(cols, upper + lower)
         return carry
 
     lax.fori_loop(0, groups, plane_group, 0)
@@ -347,11 +343,11 @@
     if relayed:
         @pl.when((here == 0) & (core == 0))
         def _():
-            pl.semaphore_signal(near_sem, inc=1, device_id={"spin": 1 - core})
+            pl.semaphore_signal(ready_sem, inc=1, device_id={"spin": 1 - core})
 
         @pl.when((here == 0) & (core == 1))
         def _():
-            pl.semaphore_wait(near_sem, 1)
+            pl.semaphore_wait(ready_sem, 1)
             for g in range(groups):
                 halo_copy(g, 1).start()
 
@@ -422,26 +418,28 @@
         behind = received[1]
         upper = subtracted(ahead, behind)
         lower = small_times(-singles[2][2:, :2], added(ahead, behind))
-        store_weave(group(g), upper + lower, False)
-
-    def rotate(g, number, dot, top):
+        rotate(g, upper + lower)
+
+    def rotate(g, full):
         cols = group(g)
-        cosine, sine = phases[number]
         for s in range(4):
             for c in range(3):
-                real = weave[0, s, c, cols, :]
-                imag = weave[1, s, c, cols, :]
-                turned_real = (cosine * real + sine * imag).astype(jnp.bfloat16)
-                turned_imag = (cosine * imag - sine * real).astype(jnp.bfloat16)
-                at = top + 2 * s * GROUP
-                rows_at = slice(at, at + GROUP)
-                rows_next = slice(at + GROUP, at + 2 * GROUP)
+                real, imag = full[s][c]
+                real = real + weave[0, s, c, cols, :]
+                imag = imag + weave[1, s, c, cols, :]
                 lanes_at = slice(c * plane, (c + 1) * plane)
                 lanes_next = slice((3 + c) * plane, (4 + c) * plane)
-                weave_mm[dot, rows_at, lanes_at] = turned_real
-                weave_mm[dot, rows_at, lanes_next] = turned_imag
-                weave_mm[dot, rows_next, lanes_at] = turned_imag
-                weave_mm[dot, rows_next, lanes_next] = -turned_real
+                for number in range(moments):
+                    cosine, sine = phases[number]
+                    turned_real = (cosine * real + sine * imag).astype(jnp.bfloat16)
+                    turned_imag = (cosine * imag - sine * real).astype(jnp.bfloat16)
+                    at = number * width + 2 * s * GROUP
+                    rows_at = slice(at, at + GROUP)
+                    rows_next = slice(at + GROUP, at + 2 * GROUP)
+                    weave_mm[g, rows_at, lanes_at] = turned_real
+                    weave_mm[g, rows_at, lanes_next] = turned_imag
+                    weave_mm[g, rows_next, lanes_at] = turned_imag
+                    weave_mm[g, rows_next, lanes_next] = -turned_real
 
     def send_far(g, number):
         pl.when(here == last)(chunk_copy(g, number, 1, True).start)
@@ -455,19 +453,20 @@
         for step in (1, last):
             pl.when(inner)(chunk_copy(g, number, step).start)
 
-    def send_rest(those):
+    def send_rest(those, phases_in=(0, 1)):
         for step in range(2, last):
             delayed = inner & (lax.rem(here + step, spaces) == far)
             for g in those:
                 for number in range(moments):
-                    pl.when(jnp.logical_not(delayed))(chunk_copy(g, number, step).start)
+                    if 0 in phases_in:
+                        pl.when(jnp.logical_not(delayed))(chunk_copy(g, number, step).start)
         for step in (1, last):
             near = here == (0 if step == 1 else last)
             for g in those:
                 for number in range(moments):
-                    pl.when(near)(chunk_copy(g, number, step).start)
-
-    width = pair.shape[-1]
+                    if 1 in phases_in:
+                        pl.when(near)(chunk_copy(g, number, step).start)
+
 
     def product(g, rows_in):
         return lax.dot_general(
@@ -497,8 +496,6 @@
 
     for g in range(groups):
         depth_group(g)
-        for number in range(moments):
-            rotate(g, number, g, number * width)
         if relayed:
             pl.when(jnp.logical_not(inner))(functools.partial(far_product, g))
             pl.when(inner)(functools.partial(full_product, g))
@@ -511,12 +508,13 @@
             for g in range(groups):
                 full_product(g)
                 if g < groups - 1:
-                    pl.when(core == 1)(functools.partial(send_rest, range(g, g + 1)))
+                    pl.when(core == 1)(functools.partial(send_rest, range(g, g + 1), (0,)))
 
     if relayed:
         @pl.when((core == 1) & jnp.logical_not(inner))
         def _():
-            pl.semaphore_wait(turn_sem, 1)
+            pl.semaphore_wait(ready_sem, 1)
+            send_rest(range(groups - 1), (1,))
             send_rest(range(groups - 1, groups))
 
         @pl.when((core == 0) | inner)
@@ -553,7 +551,7 @@
 
         @pl.when((core == 0) & jnp.logical_not(inner))
         def _():
-            pl.semaphore_signal(turn_sem, inc=1, device_id={"spin": 1 - core})
+            pl.semaphore_signal(ready_sem, inc=1, device_id={"spin": 1 - core})
 
     for number in range(moments):
         if number == 0:
@@ -667,8 +665,6 @@
             pltpu.SemaphoreType.DMA((moments,)),
             pltpu.SemaphoreType.DMA((groups, moments)),
             pltpu.SemaphoreType.REGULAR,
-            pltpu.SemaphoreType.REGULAR,
-            pltpu.SemaphoreType.REGULAR,
         ],
         compiler_params=pltpu.CompilerParams(collective_id=0, has_side_effects=True),
     )(back, fwd, link, momenta, gamma_list)

time: 18.9 us -> 18.9 us (level)
  no operation moved by 1% of the time
where the time goes in v5:
time: 18.9 us; the launch traced here: 18.7 us
  Pallas kernels  18.7 us (99%)
    pallas_call x1, Pallas kernels, body(): pl.pallas_call(functools.partial(kernel, spaces, LX, full_z, scaling), ou...  17.8 us
    pallas_call x1, Pallas kernels, body(): pl.pallas_call(store_kernel, out_shape=jax.ShapeDtypeStruct(out_shape, jn...  0.9 us

profile of v5, /device:TPU:0, one launch (start us, length us, event | category | flops | bytes accessed | tf_op | source)
XLA Modules:
  0.0 18.7 jit_solution(1879060673362769536)
XLA Ops:
  0.0 17.8 %shard_map.55.value_ref = f32[2,3,16,16,32]{4,3,2,1,0:T(8,128)S(1)} custom-call(bf16[2,4,3,32,128]{4,3,2,1,0:T(8,128)(2,1)} %bitcast.18, bf16[2,4,3,32,128]{4,3,2,1,0:T(8,128)(2,1)} %bitcast.19, bf16[3,3,3,2,128]{4,3,2,1,0:T(2,128)(2,1)} %bitcast.20, s32[3,3]{1,0:T(4,128)} %momenta_hbm.1, s32[16]{0:T(128)} %gamma_hbm.1), custom_call_target="tpu_custom_call" | custom-call | tf_op jit(solution)/shard_map/pallas_call | solution.py:636
  17.8 0.9 %shard_map.56 = f32[2,3,16,16,32]{4,3,2,1,0:T(8,128)} custom-call(f32[2,3,16,16,32]{4,3,2,1,0:T(8,128)S(1)} %shard_map.55.value_ref), custom_call_target="tpu_custom_call" | custom-call | tf_op jit(solution)/shard_map/pallas_call | solution.py:671

commit v6 on v5

--- a/solution.py
+++ b/solution.py
@@ -164,13 +164,13 @@
         for g in range(groups):
             for number in range(moments):
 
-                @pl.when(here == 0)
+                @pl.when((here == 0) & ((core == 1) if g == groups - 1 else (core >= 0)))
                 def _(g=g, number=number):
-                    chunk_recv[number, g, 0] = jnp.zeros_like(chunk_recv[number, g, 0])
+                    chunk_recv[number, g * last] = jnp.zeros_like(chunk_recv[number, 0])
 
                 @pl.when(here == last)
                 def _(g=g, number=number):
-                    chunk_recv[number, g, last - 1] = jnp.zeros_like(chunk_recv[number, g, 0])
+                    chunk_recv[number, g * last + last - 1] = jnp.zeros_like(chunk_recv[number, 0])
 
     for load in loads[:2]:
         load.wait()
@@ -355,6 +355,7 @@
     arrange(1 - core, other_back)
 
     inner = (here != 0) & (here != last)
+    waiting = (here == last - 1) & (core == 0)
     far = jnp.where(2 * here < spaces, last, 0)
 
     def chunk_copy(g, number, step, relay=False):
@@ -366,13 +367,22 @@
             target_ref, recv_sem = relay_recv.at[g, number], relay_sems.at[g, number]
         else:
             target = owner
-            target_ref, recv_sem = chunk_recv.at[number, g, step - 1], chunk_recv_sems.at[number]
+            target_ref, recv_sem = chunk_recv.at[number, g * last + step - 1], chunk_recv_sems.at[number]
         return pltpu.make_async_remote_copy(
             src_ref=source_ref,
             dst_ref=target_ref,
             send_sem=chunk_send_sem,
             recv_sem=recv_sem,
             device_id={"space": target},
+        )
+
+    def far_copy(g, number):
+        return pltpu.make_async_remote_copy(
+            src_ref=far_send.at[g, number],
+            dst_ref=chunk_recv.at[number, g * last],
+            send_sem=chunk_send_sem,
+            recv_sem=chunk_recv_sems.at[number],
+            device_id={"space": 0},
         )
 
     def wait_all(ref, send_sem, recv_sem):
@@ -386,16 +396,17 @@
         return copy
 
     def wait_chunks(number):
-        def wait(first, end):
-            ref = chunk_recv.at[number, :, first:end]
+        def wait(chunks):
+            ref = chunk_recv.at[number, :chunks]
             wait_all(ref, chunk_send_sem, chunk_recv_sems.at[number]).wait_recv()
 
         if not relayed:
-            wait(0, last)
+            wait(groups * last)
             return
-        pl.when(inner)(functools.partial(wait, 0, last))
-        pl.when(here == 0)(functools.partial(wait, 1, last))
-        pl.when(here == last)(functools.partial(wait, 0, last - 1))
+        pl.when(inner)(functools.partial(wait, groups * last))
+        pl.when((here == 0) & (core == 0))(functools.partial(wait, groups * last - groups + 1))
+        pl.when((here == 0) & (core == 1))(functools.partial(wait, groups * last - groups))
+        pl.when(here == last)(functools.partial(wait, groups * last - groups))
 
     chunk_rows = 4 * rows
     order = sorted(range(1, spaces), key=lambda step: -min(step, spaces - step))
@@ -442,16 +453,22 @@
                     weave_mm[g, rows_next, lanes_next] = -turned_real
 
     def send_far(g, number):
-        pl.when(here == last)(chunk_copy(g, number, 1, True).start)
         pl.when(here == 0)(chunk_copy(g, number, last, True).start)
+        if g < groups - 1:
+            pl.when(here == last)(chunk_copy(g, number, 1, True).start)
+        else:
+            pl.when((here == last) & (core == 1))(chunk_copy(g, number, 1, True).start)
+            pl.when((here == last) & (core == 0))(far_copy(g, number).start)
 
     def send_first(g, number):
         if not relayed:
             for step in order:
                 chunk_copy(g, number, step).start()
             return
-        for step in (1, last):
-            pl.when(inner)(chunk_copy(g, number, step).start)
+        pl.when(inner)(chunk_copy(g, number, 1).start)
+        pl.when(inner & jnp.logical_not(waiting))(chunk_copy(g, number, last).start)
+        if g == groups - 1:
+            pl.when(waiting)(chunk_copy(g, number, 2).start)
 
     def send_rest(those, phases_in=(0, 1)):
         for step in range(2, last):
@@ -526,7 +543,7 @@
             for number in range(moments):
                 for step in range(2, last):
 
-                    @pl.when(((here == 1) & (step == last - 1)) | ((here == last - 1) & (step == 2)))
+                    @pl.when(((here == 1) & (step == last - 1)) | ((here == last - 1) & (step == 2) & ((core == 1) if g == groups - 1 else (core >= 0))))
                     def _(g=g, number=number, step=step):
                         chunk_copy(g, number, last, True).wait_recv()
                         target = lax.rem(here + step, spaces)
@@ -539,8 +556,16 @@
     def summed_piece(g, number):
         total = pair[g, number, here]
         for step in range(1, spaces):
-            total = total + chunk_recv[number, g, step - 1].astype(jnp.float32)
+            total = total + chunk_recv[number, g * last + step - 1].astype(jnp.float32)
         return total * scaling
+
+    if relayed:
+
+        @pl.when(waiting)
+        def _():
+            for g in range(groups):
+                for number in range(moments):
+                    chunk_copy(g, number, last).start()
 
     lane = lax.broadcasted_iota(jnp.int32, (rows, width), 1)
     slot = lax.div(lax.rem(lane, groups * GROUP), GROUP)
@@ -655,7 +680,7 @@
             pltpu.VMEM((groups, moments, spaces, 4 * rows, width), jnp.float32),
             pltpu.VMEM((groups, moments, spaces, 4 * rows, width), jnp.bfloat16),
             pltpu.VMEM((groups, moments, 4 * rows, width), jnp.bfloat16),
-            pltpu.VMEM((moments, groups, spaces - 1, 4 * rows, width), jnp.bfloat16),
+            pltpu.VMEM((moments, groups * (spaces - 1), 4 * rows, width), jnp.bfloat16),
             pltpu.VMEM((groups, moments, 4 * rows, width), jnp.bfloat16),
             pltpu.SemaphoreType.DMA((5,)),
             pltpu.SemaphoreType.DMA((2,)),

time: 18.9 us -> 18.5 us (0.979)
  Pallas kernels: 18.7 us -> 18.3 us
    pallas_call x1, Pallas kernels: 17.8 us -> 17.4 us  [body(): pl.pallas_call(functools.partial(kernel, spaces, LX, full_z, scaling), ou...]
where the time goes in v6:
time: 18.5 us; the launch traced here: 18.4 us
  Pallas kernels  18.3 us (99%)
    pallas_call x1, Pallas kernels, body(): pl.pallas_call(functools.partial(kernel, spaces, LX, full_z, scaling), ou...  17.4 us
    pallas_call x1, Pallas kernels, body(): pl.pallas_call(store_kernel, out_shape=jax.ShapeDtypeStruct(out_shape, jn...  0.9 us

profile of v6, /device:TPU:0, one launch (start us, length us, event | category | flops | bytes accessed | tf_op | source)
XLA Modules:
  0.0 18.4 jit_solution(15189555620318450063)
XLA Ops:
  0.0 17.4 %shard_map.55.value_ref = f32[2,3,16,16,32]{4,3,2,1,0:T(8,128)S(1)} custom-call(bf16[2,4,3,32,128]{4,3,2,1,0:T(8,128)(2,1)} %bitcast.18, bf16[2,4,3,32,128]{4,3,2,1,0:T(8,128)(2,1)} %bitcast.19, bf16[3,3,3,2,128]{4,3,2,1,0:T(2,128)(2,1)} %bitcast.20, s32[3,3]{1,0:T(4,128)} %momenta_hbm.1, s32[16]{0:T(128)} %gamma_hbm.1), custom_call_target="tpu_custom_call" | custom-call | tf_op jit(solution)/shard_map/pallas_call | solution.py:661
  17.4 0.9 %shard_map.56 = f32[2,3,16,16,32]{4,3,2,1,0:T(8,128)} custom-call(f32[2,3,16,16,32]{4,3,2,1,0:T(8,128)S(1)} %shard_map.55.value_ref), custom_call_target="tpu_custom_call" | custom-call | tf_op jit(solution)/shard_map/pallas_call | solution.py:696

commit v7 on v6

--- a/solution.py
+++ b/solution.py
@@ -538,6 +538,10 @@
         def _():
             send_rest(range(groups))
 
+        @pl.when((core == 0) & (here == 0))
+        def _():
+            pl.semaphore_signal(ready_sem, inc=1, device_id={"spin": 1 - core})
+
     if relayed:
         for g in range(groups):
             for number in range(moments):
@@ -574,7 +578,7 @@
     wait_all(chunk_send.at[:, :, :last], chunk_send_sem, chunk_recv_sems.at[0]).wait_send()
     if relayed:
 
-        @pl.when((core == 0) & jnp.logical_not(inner))
+        @pl.when((core == 0) & (here == last))
         def _():
             pl.semaphore_signal(ready_sem, inc=1, device_id={"spin": 1 - core})
 

time: 18.5 us -> 18.5 us (level)
  no operation moved by 1% of the time
where the time goes in v7:
time: 18.5 us; the launch traced here: 18.4 us
  Pallas kernels  18.4 us (99%)
    pallas_call x1, Pallas kernels, body(): pl.pallas_call(functools.partial(kernel, spaces, LX, full_z, scaling), ou...  17.4 us
    pallas_call x1, Pallas kernels, body(): pl.pallas_call(store_kernel, out_shape=jax.ShapeDtypeStruct(out_shape, jn...  0.9 us

profile of v7, /device:TPU:0, one launch (start us, length us, event | category | flops | bytes accessed | tf_op | source)
XLA Modules:
  0.0 18.4 jit_solution(8016985501350695958)
XLA Ops:
  0.0 17.4 %shard_map.55.value_ref = f32[2,3,16,16,32]{4,3,2,1,0:T(8,128)S(1)} custom-call(bf16[2,4,3,32,128]{4,3,2,1,0:T(8,128)(2,1)} %bitcast.18, bf16[2,4,3,32,128]{4,3,2,1,0:T(8,128)(2,1)} %bitcast.19, bf16[3,3,3,2,128]{4,3,2,1,0:T(2,128)(2,1)} %bitcast.20, s32[3,3]{1,0:T(4,128)} %momenta_hbm.1, s32[16]{0:T(128)} %gamma_hbm.1), custom_call_target="tpu_custom_call" | custom-call | tf_op jit(solution)/shard_map/pallas_call | solution.py:665
  17.5 0.9 %shard_map.56 = f32[2,3,16,16,32]{4,3,2,1,0:T(8,128)} custom-call(f32[2,3,16,16,32]{4,3,2,1,0:T(8,128)S(1)} %shard_map.55.value_ref), custom_call_target="tpu_custom_call" | custom-call | tf_op jit(solution)/shard_map/pallas_call | solution.py:700
